TPU v7x, 8 devices: a whole 2x2x1 slice. The times are simulated.
8 devices in a mesh: by: 2 (over z, y), bx: 4 (over x, core).
Axes of the slice: x: 2, y: 2, z: 1, core: 2. Of those that a mesh axis runs over, the one named last changes fastest.
Arguments:
- wave_fn: float32 [512, 4, 4, 512], P('bx', None, None, 'by')
- left_env: float32 [512, 4, 512], P('bx')
- mpo_ten: float32 [4, 4, 4, 4], replicated
- right_env: float32 [512, 4, 512], P('by')
Outputs:
- output: float32 [512, 4, 4, 512], P('bx', None, None, 'by')
All inputs are finite; a program needn't handle non-finite values.
Results may differ from a plain program's by a relative error of at most 0.001.
Values sent between devices are 32-bit elements.
A program may use at most 1 GiB of HBM per device.

v0:
```python
import jax
import jax.numpy as jnp
from jax import lax
from jax.sharding import PartitionSpec as P


def solution(mesh):
    prec_mode = lax.Precision.HIGHEST

    def local_apply(wave_blk, left_rows, mpo_ten, right_rows):
        row_share, mpo_dim, bond_dim = left_rows.shape
        phys_dim = wave_blk.shape[1]
        col_share = wave_blk.shape[3]
        wave_cols = lax.all_gather(wave_blk, 'bx', axis=0, tiled=True)
        stage_one = jnp.dot(left_rows.reshape(row_share * mpo_dim, bond_dim), wave_cols.reshape(bond_dim, phys_dim * phys_dim * col_share), precision=prec_mode, preferred_element_type=jnp.float32)
        stage_one = stage_one.reshape(row_share, mpo_dim, phys_dim, phys_dim, col_share)
        stage_two = jnp.einsum('aupqf,uspv->asvqf', stage_one, mpo_ten, precision=prec_mode, preferred_element_type=jnp.float32)
        stage_three = jnp.einsum('asvqf,vtqr->astrf', stage_two, mpo_ten, precision=prec_mode, preferred_element_type=jnp.float32)
        right_cols = lax.all_to_all(right_rows, 'by', 2, 0, tiled=True)
        part_sum = lax.dot_general(stage_three.reshape(row_share * phys_dim * phys_dim, mpo_dim * col_share), right_cols.reshape(bond_dim, mpo_dim * col_share), (((1,), (1,)), ((), ())), precision=prec_mode, preferred_element_type=jnp.float32)
        part_sum = part_sum.reshape(row_share, phys_dim, phys_dim, bond_dim)
        return lax.psum_scatter(part_sum, 'by', scatter_dimension=3, tiled=True)

    return jax.shard_map(local_apply, mesh=mesh, in_specs=(P('bx', None, None, 'by'), P('bx', None, None), P(), P('by', None, None)), out_specs=P('bx', None, None, 'by'), check_vma=False)
```

profile of v0, /device:TPU:0, one launch (start us, length us, event | category | flops | bytes accessed | tf_op | source)
XLA Modules:
  0.0 228.4 jit_solution(5172392079378154419)
XLA Ops:
  6.5 0.0 copy-start
  6.5 0.0 all-gather.2.cloned.1.call-start
  6.5 0.7 all-gather.2.cloned.1.call-update
  7.3 0.0 reduce-scatter.2.cloned.1.call-start
  7.3 4.1 %copy.19 = f32[256,4,512]{0,1,2:T(4,128)} copy(f32[256,4,512]{2,1,0:T(4,128)} %param.7) | data formatting | bytes 4194304 | tf_op args[3]
  11.4 30.3 %all_to_all.15 = f32[256,4,512]{0,1,2:T(4,128)S(1)} all-to-all(f32[256,4,512]{0,1,2:T(4,128)} %copy.19), channel_id=1, replica_groups=mesh['by'=2,'bx'=4] {'by'}, dimensions={2} | all-to-all | bytes 4194304 | tf_op jit(solution)/shard_map/all_to_all | solution.py:19
  41.7 2.5 %copy.20 = f32[256,4,2,256]{3,1,0,2:T(4,128)} copy(f32[256,4,2,256]{0,1,3,2:T(4,128)S(1)} %bitcast.42) | data formatting | bytes 4194304 | tf_op jit(solution)/shard_map/all_to_all | solution.py:19
  44.2 2.3 %reshape.26 = f32[512,1024,1,1]{1,0,2,3:T(8,128)S(1)} reshape(f32[2,256,4,256]{3,2,1,0:T(4,128)} %bitcast.43) | data formatting | bytes 4194304 | tf_op jit(solution)/shard_map/reshape | solution.py:20
  46.5 0.0 copy-start.1
  46.5 20.9 %all-gather.2.cloned.1.call-done = f32[512,4,4,256]{3,2,1,0:T(4,128)} async-done(((f32[128,4,4,256]{3,2,1,0:T(4,128)}), f32[512,4,4,256]{3,2,1,0:T(4,128)}) %all-gather.2.cloned.1.call-update) | async-done | bytes 8388624 | tf_op jit(solution)/shard_map/all_gather | solution.py:14
  67.4 9.9 %copy.33 = f32[512,4,4,256]{0,3,2,1:T(8,128)} copy(f32[512,4,4,256]{3,2,1,0:T(4,128)} %all-gather.2.cloned.1.call-done) | data formatting | bytes 16777216 | tf_op jit(solution)/shard_map/reshape | solution.py:15
  77.4 0.0 copy-done.1
  77.4 16.7 %fusion.11 = f32[128,4,4,4,256,1]{4,0,3,2,1,5:T(8,128)S(1)} fusion(f32[512,4,4,256]{0,3,2,1:T(8,128)} %copy.33, f32[128,4,512,1,1]{2,1,0,4,3:T(4,128)S(1)} %bitcast.44), kind=kOutput, calls=%fused_computation.9 | convolution fusion | flops 12884901888 | bytes 17825792 | tf_op jit(solution)/shard_map/dot_general | solution.py:15
  94.0 0.0 copy-done
  94.0 21.9 %fusion.4 = f32[128,4,256,4,4,1]{2,4,5,1,3,0:T(4,128)S(1)} fusion(f32[128,4,4,4,256,1]{4,0,3,2,1,5:T(8,128)S(1)} %fusion.11, f32[4,4,4,4]{3,2,1,0:T(4,128)S(1)} %copy-done), kind=kOutput, calls=%fused_computation.4 | convolution fusion | flops 402653184 | bytes 16778240 | tf_op jit(solution)/shard_map/aupqf,uspv->asvqf/dot_general | solution.py:17
  116.0 16.8 %fusion.8 = f32[128,4,4,4,256]{4,3,2,1,0:T(4,128)} fusion(f32[128,4,256,4,4,1]{2,4,5,1,3,0:T(4,128)S(1)} %fusion.4, f32[4,4,4,4,1,1]{3,2,1,0,5,4:T(4,128)S(1)} %bitcast.41), kind=kOutput, calls=%fused_computation.8 | convolution fusion | flops 402653184 | bytes 16778240 | tf_op jit(solution)/shard_map/asvqf,vtqr->astrf/dot_general | solution.py:18
  132.8 10.9 %dot_general.23 = f32[128,4,4,1024]{3,2,1,0:T(4,128)} reshape(f32[128,4,4,4,256]{4,3,2,1,0:T(4,128)} %fusion.8) | data formatting | bytes 16777216 | tf_op jit(solution)/shard_map/dot_general | solution.py:20
  143.7 21.9 %fusion.6 = f32[128,4,4,512]{3,0,2,1:T(8,128)} fusion(f32[128,4,4,1024]{3,2,1,0:T(4,128)} %dot_general.23, f32[512,1024,1,1]{1,0,2,3:T(8,128)S(1)} %reshape.26), kind=kOutput, calls=%fused_computation.6 | convolution fusion | flops 12884901888 | bytes 14680064 | tf_op jit(solution)/shard_map/dot_general | solution.py:20
  165.6 0.0 reduce-scatter.2.cloned.1.call-update
  165.7 51.6 %reduce-scatter.2.cloned.1.call-done = f32[128,4,4,256]{3,0,2,1:T(8,128)} async-done(((f32[128,4,4,512]{3,0,2,1:T(8,128)}), f32[128,4,4,256]{3,0,2,1:T(8,128)}) %reduce-scatter.2.cloned.1.call-update) | async-done | bytes 2097168 | tf_op jit(solution)/shard_map/reduce_scatter | solution.py:22
  217.3 4.3 %copy.22 = f32[128,4,4,256]{3,2,1,0:T(4,128)} copy(f32[128,4,4,256]{3,0,2,1:T(8,128)} %reduce-scatter.2.cloned.1.call-done) | data formatting | bytes 4194304 | tf_op jit(solution)/shard_map/reduce_scatter | solution.py:22
Async XLA Ops:
  6.5 87.5 %copy-start = (f32[4,4,4,4]{3,2,1,0:T(4,128)S(1)}, f32[4,4,4,4]{3,2,1,0:T(4,128)}, u32[]{:S(2)}) copy-start(f32[4,4,4,4]{3,2,1,0:T(4,128)} %param.6) | copy-start | bytes 3076
  6.5 60.9 %all-gather.2.cloned.1.call-start = ((), (), s32[]{:S(2)}) async-start(), calls=%async_computation.2 | async-start | bytes 10485760 | tf_op jit(solution)/shard_map/all_gather | solution.py:14
  7.3 210.0 %reduce-scatter.2.cloned.1.call-start = ((), (), s32[]{:S(2)}) async-start(), calls=%async_computation.3 | async-start | bytes 6291456 | tf_op jit(solution)/shard_map/reduce_scatter | solution.py:22
  46.5 30.8 %copy-start.1 = (f32[128,4,512]{2,1,0:T(4,128)S(1)}, f32[128,4,512]{2,1,0:T(4,128)}, u32[]{:S(2)}) copy-start(f32[128,4,512]{2,1,0:T(4,128)} %param.5) | copy-start | bytes 3145732
Sparse Core Ops, SparseCore 0:
  8.9 58.5 all-gather.1
  165.8 51.4 reduce-scatter.1
where the time goes:
time: 229 us; the launch traced here: 228 us
  matrix products  77.3 us (34%)
  waiting for transfers between devices  73.3 us (32%)
  local copies, waits for them, and re-layouts  34 us (15%)
  blocking collectives  30.3 us (13%)
  between operations  13.4 us (6%)
    reduce_scatter x1, waiting for transfers between devices, local_apply(): return lax.psum_scatter(part_sum, 'by', scatter_dimension=3, tiled=True)  51.6 us
    all_to_all x1, blocking collectives, local_apply(): right_cols = lax.all_to_all(right_rows, 'by', 2, 0, tiled=True)  30.3 us
    dot_general x1, matrix products, local_apply(): lax.dot_general(stage_three.reshape(row_share * phys_dim * phys_dim, mpo_...  21.9 us
    dot_general x1, matrix products, local_apply(): jnp.einsum('aupqf,uspv->asvqf', stage_one, mpo_ten, precision=prec_mode,...  21.9 us
    all_gather x1, waiting for transfers between devices, local_apply(): wave_cols = lax.all_gather(wave_blk, 'bx', axis=0, tiled=True)  20.9 us
    dot_general x1, matrix products, local_apply(): jnp.einsum('asvqf,vtqr->astrf', stage_two, mpo_ten, precision=prec_mode,...  16.8 us
    dot_general x1, matrix products, local_apply(): jnp.dot(left_rows.reshape(row_share * mpo_dim, bond_dim), wave_cols.resha...  16.7 us
    dot_general x1, local copies, waits for them, and re-layouts, local_apply(): lax.dot_general(stage_three.reshape(row_share * phys_dim * phys_dim, mpo_...  10.9 us
  transfers between devices with their start and end apart: 2, of which 2 were waited for; matrix products, arithmetic and copies ran while one was open for 4% of the time, Pallas kernels for 0%

commit v1 on v0

v1 whole, which is shorter than its diff:
```python
import functools

import jax
import jax.numpy as jnp
from jax import lax
from jax.experimental import pallas as pl
from jax.experimental.pallas import tpu as pltpu
from jax.sharding import PartitionSpec as P

HI = lax.Precision.HIGHEST
F32 = jnp.float32
LANE = 128
T1_PQ = 4
T3_GROUPS = 4
Y_ROWS = 1024
OWN, OTHER = 0, 1


def dot(a, b):
    return jnp.dot(a, b, precision=HI, preferred_element_type=F32)


def kernel(x_ref, l_ref, w_ref, r_ref, y_ref, xg, ln, l2, rn, rt, t1s, t3s, ys, yo, kron, wa, wb, scale, load_sem, env_sem, out_sem, send_sem, recv_sem):
    by = lax.axis_index('by')
    bx = lax.axis_index('bx')
    core = lax.rem(bx, 2)
    chip = bx // 2
    sib = {'by': by, 'bx': bx + 1 - 2 * core}
    xnb = {'by': by, 'bx': lax.rem(bx + 2, 4)}
    ynb = {'by': 1 - by, 'bx': bx}

    loads = []
    for h in range(2):
        for pq in range(16):
            loads.append(pltpu.make_async_copy(
                x_ref.at[:, pq // 4, pq % 4, pl.ds(h * LANE, LANE)],
                xg.at[OWN, h, OWN, core, pq], load_sem.at[h, pq]))
    for cp in loads:
        cp.start()
    env = []
    for half in range(2):
        for k in range(2):
            c0 = ((chip + half) % 2 * 2 + k) * LANE
            env.append(pltpu.make_async_copy(
                l_ref.at[:, :, pl.ds(pl.multiple_of(c0, LANE), LANE)], ln.at[half, k], env_sem.at[half * 2 + k]))
    for half in range(2):
        for h in range(2):
            f0 = ((by + half) % 2 * 2 + h) * LANE
            for r in range(4):
                env.append(pltpu.make_async_copy(
                    r_ref.at[:, r, pl.ds(pl.multiple_of(f0, LANE), LANE)], rn.at[half * 2 + h, r],
                    env_sem.at[4 + (half * 2 + h) * 4 + r]))
    for cp in env:
        cp.start()

    barrier = pltpu.get_barrier_semaphore()
    for d in (sib, xnb, ynb):
        pl.semaphore_signal(barrier, inc=1, device_id=d, device_id_type=pl.DeviceIdType.MESH)
    pl.semaphore_wait(barrier, 3)

    sends = []

    def send(src, dst, k, h, pp, to):
        n = len(sends)
        cp = pltpu.make_async_remote_copy(
            src_ref=xg.at[src[0], h, src[1], k, pl.ds(pp * 8, 8)],
            dst_ref=xg.at[dst[0], h, dst[1], k, pl.ds(pp * 8, 8)],
            send_sem=send_sem.at[n],
            recv_sem=recv_sem.at[dst[0], h, dst[1], k, pp],
            device_id=to, device_id_type=pl.DeviceIdType.MESH)
        cp.start()
        sends.append(cp)

    def arrived(slot, k, h, pp):
        ref = xg.at[slot[0], h, slot[1], k, pl.ds(pp * 8, 8)]
        pltpu.make_async_copy(ref, ref, recv_sem.at[slot[0], h, slot[1], k, pp]).wait()

    me, x_slot, y_slot, d_slot = (OWN, OWN), (OWN, OTHER), (OTHER, OWN), (OTHER, OTHER)
    for h in range(2):
        for pp in range(2):
            for cp in loads[h * 16 + pp * 8:h * 16 + pp * 8 + 8]:
                cp.wait()
            send(me, x_slot, core, h, pp, xnb)
            send(me, y_slot, core, h, pp, ynb)
            send(me, me, core, h, pp, sib)

    def relay(h, pp):
        arrived(x_slot, core, h, pp)
        send(x_slot, x_slot, core, h, pp, sib)
        if pp == 0:
            send(x_slot, d_slot, core, h, pp, ynb)
        arrived(y_slot, core, h, pp)
        send(y_slot, y_slot, core, h, pp, sib)
        if pp == 1:
            send(y_slot, d_slot, core, h, pp, xnb)

    def relay_diag(h):
        for pp in range(2):
            arrived(d_slot, core, h, pp)
            send(d_slot, d_slot, core, h, pp, sib)

    for cp in env[:4]:
        cp.wait()
    for half in range(2):
        for k in range(2):
            l2[half, :, k * LANE:(k + 1) * LANE] = ln[half, k].reshape(512, LANE)
    wa[...] = jnp.zeros_like(wa)
    wb[...] = jnp.zeros_like(wb)
    lane8 = lax.broadcasted_iota(jnp.int32, (8, LANE), 1)
    row8 = lax.broadcasted_iota(jnp.int32, (8, LANE), 0)
    lane16 = lax.broadcasted_iota(jnp.int32, (16, LANE), 1)
    row16 = lax.broadcasted_iota(jnp.int32, (16, LANE), 0)

    def fill(i, carry):
        va, vb = carry
        i0, i1, i2 = i // 16, i // 4 % 4, i % 4
        for i3 in range(4):
            val = w_ref[i0, i1, i2, i3]
            va = jnp.where((row8 == i1) & (lane8 == i0 * 16 + i2 * 4 + i3), val, va)
            vb = jnp.where((row16 == i3 * 4 + i1) & (lane16 == i0 * 4 + i2), val, vb)
        return va, vb

    va, vb = lax.fori_loop(0, 64, fill, (jnp.zeros((8, LANE), F32), jnp.zeros((16, LANE), F32)))
    top = jnp.max(jnp.max(jnp.abs(va), axis=1, keepdims=True), axis=0, keepdims=True)
    scale[...] = jnp.broadcast_to(top, scale.shape)
    wa[...] = va / scale[...]
    wb[...] = vb / jnp.broadcast_to(top, (16, LANE))

    row = lax.broadcasted_iota(jnp.int32, (256, LANE), 0)
    a_mat = jnp.zeros((256, LANE), F32)
    for s in range(4):
        a_mat = jnp.where(row // 4 % 4 == s, wa[s:s + 1, :], a_mat)
    c_mat = jnp.zeros((256, LANE), F32)
    for rt_ in range(16):
        c_mat = jnp.where((row // 64) * 4 + row % 4 == rt_, wb[rt_:rt_ + 1, :], c_mat)
    col = lax.broadcasted_iota(jnp.int32, (LANE, 256), 1)
    pick = lax.broadcasted_iota(jnp.int32, (LANE, 256), 0)
    total = jnp.zeros((256, 256), F32)
    for v in range(4):
        left = dot(a_mat, jnp.where(pick == col % 4 * 16 + col // 64 * 4 + v, 1.0, 0.0).astype(F32))
        right = dot(c_mat, jnp.where(pick == v * 4 + col // 16 % 4, 1.0, 0.0).astype(F32))
        total = total + left * right
    krow = lax.broadcasted_iota(jnp.int32, (256, 256), 0)
    kcol = lax.broadcasted_iota(jnp.int32, (256, 256), 1)
    kron[...] = jnp.where(krow // 16 % 4 == kcol // 4 % 4, total, 0.0)
    for cp in env[4:]:
        cp.wait()
    for fc in range(4):
        for r in range(4):
            rt[fc, r * LANE:(r + 1) * LANE, :] = rn[fc, r].T

    def stage1(slot, h, pp, first):
        fh, ch = slot
        buf = fh * 2 + h

        def body(j, _):
            pq = pp * 8 + T1_PQ * j
            xs = jnp.concatenate([
                jnp.concatenate([xg[fh, h, ch, k, pq + n] for n in range(T1_PQ)], axis=1) for k in range(2)], axis=0)
            t = dot(l2[ch], xs)
            for ab in range(2):
                for n in range(T1_PQ):
                    dst = (buf, slice(None), pl.ds(pl.multiple_of((pq + n) * 16, 16), 16), slice(ab * LANE, (ab + 1) * LANE))
                    part = t[ab * 256:(ab + 1) * 256, n * LANE:(n + 1) * LANE].reshape(16, 16, LANE)
                    t1s[dst] = part if first else t1s[dst] + part
            return 0

        lax.fori_loop(0, 8 // T1_PQ, body, 0)

    def stage23(fh, h, first, final):
        buf = fh * 2 + h
        sc = scale[0:1, 0:1]

        def body(i, _):
            ts = jnp.concatenate([t1s[buf, i * T3_GROUPS + g] for g in range(T3_GROUPS)], axis=1)
            t = dot(kron[...], ts * sc) * sc
            for g in range(T3_GROUPS):
                for ab in range(2):
                    lanes = slice(g * 256 + ab * LANE, g * 256 + (ab + 1) * LANE)
                    rows = pl.ds(pl.multiple_of(ab * 1024 + (i * T3_GROUPS + g) * 64, 64), 64)
                    for r in range(4):
                        t3s[rows, r * LANE:(r + 1) * LANE] = t[r * 64:(r + 1) * 64, lanes]
            return 0

        lax.fori_loop(0, 16 // T3_GROUPS, body, 0)

        def last(i, _):
            rows = pl.ds(pl.multiple_of(i * Y_ROWS, Y_ROWS), Y_ROWS)
            t = dot(t3s[rows, :], rt[buf])
            for b in range(2):
                part = t[:, b * LANE:(b + 1) * LANE]
                if not first:
                    part = ys[b, rows, :] + part
                if final:
                    yo[b, pl.ds(i * (Y_ROWS // 16), Y_ROWS // 16)] = part.reshape(Y_ROWS // 16, 4, 4, LANE)
                    out_copy(b, i).start()
                else:
                    ys[b, rows, :] = part
            return 0

        lax.fori_loop(0, 2048 // Y_ROWS, last, 0)

    def out_copy(b, i):
        part = pl.ds(i * (Y_ROWS // 16), Y_ROWS // 16)
        return pltpu.make_async_copy(yo.at[b, part], y_ref.at[part, :, :, pl.ds(b * LANE, LANE)], out_sem.at[b, i])

    other_core = 1 - core
    for h in range(2):
        for pp in range(2):
            arrived(me, other_core, h, pp)
            stage1(me, h, pp, True)
    for h in range(2):
        for pp in range(2):
            relay(h, pp)
            arrived(x_slot, other_core, h, pp)
            stage1(x_slot, h, pp, False)
            arrived(y_slot, other_core, h, pp)
            stage1(y_slot, h, pp, True)
        stage23(OWN, h, h == 0, False)
    for h in range(2):
        relay_diag(h)
        for pp in range(2):
            arrived(d_slot, other_core, h, pp)
            stage1(d_slot, h, pp, False)
        stage23(OTHER, h, False, h == 1)

    for i in range(2048 // Y_ROWS):
        for b in range(2):
            out_copy(b, i).wait()
    for cp in sends:
        cp.wait_send()


def solution(mesh):
    def local_apply(x, left, mpo, right):
        any_spec = pl.BlockSpec(memory_space=pl.ANY)
        return pl.pallas_call(
            kernel,
            out_shape=jax.ShapeDtypeStruct((128, 4, 4, 256), F32),
            in_specs=[any_spec, any_spec, pl.BlockSpec(memory_space=pltpu.SMEM), any_spec],
            out_specs=any_spec,
            scratch_shapes=[
                pltpu.VMEM((2, 2, 2, 2, 16, 128, LANE), F32),
                pltpu.VMEM((2, 2, 128, 4, LANE), F32),
                pltpu.VMEM((2, 512, 256), F32),
                pltpu.VMEM((4, 4, 256, LANE), F32),
                pltpu.VMEM((4, 512, 256), F32),
                pltpu.VMEM((4, 16, 256, 256), F32),
                pltpu.VMEM((2048, 512), F32),
                pltpu.VMEM((2, 2048, LANE), F32),
                pltpu.VMEM((2, 128, 4, 4, LANE), F32),
                pltpu.VMEM((256, 256), F32),
                pltpu.VMEM((8, LANE), F32),
                pltpu.VMEM((16, LANE), F32),
                pltpu.VMEM((8, LANE), F32),
                pltpu.SemaphoreType.DMA((2, 16)),
                pltpu.SemaphoreType.DMA((20,)),
                pltpu.SemaphoreType.DMA((2, 2048 // Y_ROWS)),
                pltpu.SemaphoreType.DMA((28,)),
                pltpu.SemaphoreType.DMA((2, 2, 2, 2, 2)),
            ],
            compiler_params=pltpu.CompilerParams(collective_id=0, has_side_effects=True, vmem_limit_bytes=62 * 2**20),
            name='two_site',
        )(x, left, mpo, right)

    return jax.shard_map(local_apply, mesh=mesh, in_specs=(P('bx', None, None, 'by'), P('bx', None, None), P(), P('by', None, None)), out_specs=P('bx', None, None, 'by'), check_vma=False)
```

time: 229 us -> 101 us (0.44)
  Pallas kernels: 0 us -> 96.6 us
  matrix products: 77.3 us -> 0 us
  waiting for transfers between devices: 73.3 us -> 0 us
  local copies, waits for them, and re-layouts: 34 us -> 3.33 us
  blocking collectives: 30.3 us -> 0 us
  between operations: 13.4 us -> 0.01 us
    pallas_call x0 -> x1, Pallas kernels: none -> 96.6 us  [local_apply(): pl.pallas_call(kernel, out_shape=jax.ShapeDtypeStruct((128, 4, 4, 256), F...]
    dot_general x4 -> x0, matrix products: 77.3 us -> none  [the longest x1 21.9 us: local_apply(): lax.dot_general(stage_three.reshape(row_share * phys_dim * phys_dim, mpo_...]
    reduce_scatter x1 -> x0, waiting for transfers between devices: 51.6 us -> none  [local_apply(): return lax.psum_scatter(part_sum, 'by', scatter_dimension=3, tiled=True)]
    all_to_all x1 -> x0, blocking collectives: 30.3 us -> none  [local_apply(): right_cols = lax.all_to_all(right_rows, 'by', 2, 0, tiled=True)]
    all_gather x1 -> x0, waiting for transfers between devices: 20.9 us -> none  [local_apply(): wave_cols = lax.all_gather(wave_blk, 'bx', axis=0, tiled=True)]
    reshape x2 -> x0, local copies, waits for them, and re-layouts: 12.3 us -> none  [the longest x1 9.93 us: local_apply(): wave_cols.reshape(bond_dim, phys_dim * phys_dim * col_share)]
    dot_general x1 -> x0, local copies, waits for them, and re-layouts: 10.9 us -> none  [local_apply(): lax.dot_general(stage_three.reshape(row_share * phys_dim * phys_dim, mpo_...]
    reduce_scatter x1 -> x0, local copies, waits for them, and re-layouts: 4.26 us -> none  [local_apply(): return lax.psum_scatter(part_sum, 'by', scatter_dimension=3, tiled=True)]
  transfers between devices with their start and end apart: 2 -> 0, of which waited for: 2 -> 0; matrix products, arithmetic and copies ran while one was open for 4% -> 0% of each run, Pallas kernels for 0% -> 0%
where the time goes in v1:
time: 101 us; the launch traced here: 99.9 us
  Pallas kernels  96.6 us (96%)
  local copies, waits for them, and re-layouts  3.33 us (3%)
    pallas_call x1, Pallas kernels, local_apply(): pl.pallas_call(kernel, out_shape=jax.ShapeDtypeStruct((128, 4, 4, 256), F...  96.6 us
    unnamed x1, local copies, waits for them, and re-layouts  3.33 us

profile of v1, /device:TPU:0, one launch (start us, length us, event | category | flops | bytes accessed | tf_op | source)
XLA Modules:
  0.0 99.9 jit_solution(7136193580779189482)
XLA Ops:
  0.0 96.6 %two_site.1 = f32[128,4,4,256]{3,2,1,0:T(4,128)} custom-call(f32[128,4,4,256]{3,2,1,0:T(4,128)} %x_ref.1, f32[128,4,512]{2,1,0:T(4,128)} %l_ref.1, f32[4,4,4,4]{3,2,1,0:T(4,128)} %w_ref.1, f32[256,4,512]{2,1,0:T(4,128)} %r_ref.1), custom_call_target="tpu_custom_call" | custom-call | tf_op jit(solution)/shard_map/two_site/pallas_call | solution.py:237
  96.6 3.3 %copy.6 = f32[128,4,4,256]{3,2,1,0:T(4,128)} copy(f32[128,4,4,256]{3,2,1,0:T(4,128)} %two_site.1) | data formatting | bytes 4194304

commit v2 on v1

--- a/solution.py
+++ b/solution.py
@@ -10,8 +10,7 @@
 HI = lax.Precision.HIGHEST
 F32 = jnp.float32
 LANE = 128
-T1_PQ = 4
-T3_GROUPS = 4
+T3_GROUPS = 8
 Y_ROWS = 1024
 OWN, OTHER = 0, 1
 
@@ -58,46 +57,39 @@
         pl.semaphore_signal(barrier, inc=1, device_id=d, device_id_type=pl.DeviceIdType.MESH)
     pl.semaphore_wait(barrier, 3)
 
-    sends = []
-
-    def send(src, dst, k, h, pp, to):
-        n = len(sends)
-        cp = pltpu.make_async_remote_copy(
-            src_ref=xg.at[src[0], h, src[1], k, pl.ds(pp * 8, 8)],
-            dst_ref=xg.at[dst[0], h, dst[1], k, pl.ds(pp * 8, 8)],
-            send_sem=send_sem.at[n],
-            recv_sem=recv_sem.at[dst[0], h, dst[1], k, pp],
+    def send(kind, h, pp):
+        fh, ch = ((0, 0), (0, 0), (0, 0), (0, 1), (1, 0), (1, 1), (pp, 1 - pp))[kind]
+        dh, dc = ((0, 1), (1, 0), (0, 0), (0, 1), (1, 0), (1, 1), (1, 1))[kind]
+        to = (xnb, ynb, sib, sib, sib, sib, {'by': lax.rem(by + 1 - pp, 2), 'bx': lax.rem(bx + 2 * pp, 4)})[kind]
+        return pltpu.make_async_remote_copy(
+            src_ref=xg.at[fh, h, ch, core, pl.ds(pp * 8, 8)],
+            dst_ref=xg.at[dh, h, dc, core, pl.ds(pp * 8, 8)],
+            send_sem=send_sem.at[kind, h, pp],
+            recv_sem=recv_sem.at[dh, h, dc, core, pp],
             device_id=to, device_id_type=pl.DeviceIdType.MESH)
-        cp.start()
-        sends.append(cp)
-
-    def arrived(slot, k, h, pp):
-        ref = xg.at[slot[0], h, slot[1], k, pl.ds(pp * 8, 8)]
-        pltpu.make_async_copy(ref, ref, recv_sem.at[slot[0], h, slot[1], k, pp]).wait()
-
-    me, x_slot, y_slot, d_slot = (OWN, OWN), (OWN, OTHER), (OTHER, OWN), (OTHER, OTHER)
+
+    def arrived(fh, ch, k, h, pp):
+        ref = xg.at[fh, h, ch, k, pl.ds(pp * 8, 8)]
+        pltpu.make_async_copy(ref, ref, recv_sem.at[fh, h, ch, k, pp]).wait()
+
     for h in range(2):
         for pp in range(2):
             for cp in loads[h * 16 + pp * 8:h * 16 + pp * 8 + 8]:
                 cp.wait()
-            send(me, x_slot, core, h, pp, xnb)
-            send(me, y_slot, core, h, pp, ynb)
-            send(me, me, core, h, pp, sib)
+            for kind in range(3):
+                send(kind, h, pp).start()
 
     def relay(h, pp):
-        arrived(x_slot, core, h, pp)
-        send(x_slot, x_slot, core, h, pp, sib)
-        if pp == 0:
-            send(x_slot, d_slot, core, h, pp, ynb)
-        arrived(y_slot, core, h, pp)
-        send(y_slot, y_slot, core, h, pp, sib)
-        if pp == 1:
-            send(y_slot, d_slot, core, h, pp, xnb)
+        arrived(OWN, OTHER, core, h, pp)
+        send(3, h, pp).start()
+        arrived(OTHER, OWN, core, h, pp)
+        send(4, h, pp).start()
+        send(6, h, pp).start()
 
     def relay_diag(h):
         for pp in range(2):
-            arrived(d_slot, core, h, pp)
-            send(d_slot, d_slot, core, h, pp, sib)
+            arrived(OTHER, OTHER, core, h, pp)
+            send(5, h, pp).start()
 
     for cp in env[:4]:
         cp.wait()
@@ -149,86 +141,108 @@
         for r in range(4):
             rt[fc, r * LANE:(r + 1) * LANE, :] = rn[fc, r].T
 
-    def stage1(slot, h, pp, first):
-        fh, ch = slot
+    def stage1(fh, ch, h, pp, first):
         buf = fh * 2 + h
-
-        def body(j, _):
-            pq = pp * 8 + T1_PQ * j
-            xs = jnp.concatenate([
-                jnp.concatenate([xg[fh, h, ch, k, pq + n] for n in range(T1_PQ)], axis=1) for k in range(2)], axis=0)
-            t = dot(l2[ch], xs)
+        xs = jnp.concatenate([
+            jnp.concatenate([xg[fh, h, ch, k, pp * 8 + n] for n in range(8)], axis=1) for k in range(2)], axis=0)
+        t = dot(l2[ch], xs)
+        for n in range(8):
+            row0 = (pp * 8 + n) * 16
+            if not isinstance(pp, int):
+                row0 = pl.multiple_of(row0, 16)
             for ab in range(2):
-                for n in range(T1_PQ):
-                    dst = (buf, slice(None), pl.ds(pl.multiple_of((pq + n) * 16, 16), 16), slice(ab * LANE, (ab + 1) * LANE))
-                    part = t[ab * 256:(ab + 1) * 256, n * LANE:(n + 1) * LANE].reshape(16, 16, LANE)
-                    t1s[dst] = part if first else t1s[dst] + part
-            return 0
-
-        lax.fori_loop(0, 8 // T1_PQ, body, 0)
-
-    def stage23(fh, h, first, final):
+                dst = (buf, slice(None), pl.ds(row0, 16), slice(ab * LANE, (ab + 1) * LANE))
+                part = t[ab * 256:(ab + 1) * 256, n * LANE:(n + 1) * LANE].reshape(16, 16, LANE)
+                t1s[dst] = part if first else t1s[dst] + part
+
+    def stage2(fh, h):
         buf = fh * 2 + h
         sc = scale[0:1, 0:1]
 
         def body(i, _):
-            ts = jnp.concatenate([t1s[buf, i * T3_GROUPS + g] for g in range(T3_GROUPS)], axis=1)
-            t = dot(kron[...], ts * sc) * sc
             for g in range(T3_GROUPS):
+                t = dot(kron[...], t1s[buf, i * T3_GROUPS + g] * sc) * sc
                 for ab in range(2):
-                    lanes = slice(g * 256 + ab * LANE, g * 256 + (ab + 1) * LANE)
                     rows = pl.ds(pl.multiple_of(ab * 1024 + (i * T3_GROUPS + g) * 64, 64), 64)
                     for r in range(4):
-                        t3s[rows, r * LANE:(r + 1) * LANE] = t[r * 64:(r + 1) * 64, lanes]
+                        t3s[rows, r * LANE:(r + 1) * LANE] = t[r * 64:(r + 1) * 64, ab * LANE:(ab + 1) * LANE]
             return 0
 
         lax.fori_loop(0, 16 // T3_GROUPS, body, 0)
 
-        def last(i, _):
+    def stage3(fh, h, between=None, final=False):
+        buf = fh * 2 + h
+
+        def body(i, _):
             rows = pl.ds(pl.multiple_of(i * Y_ROWS, Y_ROWS), Y_ROWS)
             t = dot(t3s[rows, :], rt[buf])
             for b in range(2):
                 part = t[:, b * LANE:(b + 1) * LANE]
-                if not first:
-                    part = ys[b, rows, :] + part
+                if fh == 0:
+                    part = part + jnp.where(h == 0, 0.0, ys[b, rows, :])
+                else:
+                    part = part + ys[b, rows, :]
                 if final:
                     yo[b, pl.ds(i * (Y_ROWS // 16), Y_ROWS // 16)] = part.reshape(Y_ROWS // 16, 4, 4, LANE)
                     out_copy(b, i).start()
                 else:
                     ys[b, rows, :] = part
+            if between is not None:
+                pl.when(i == 0)(between)
             return 0
 
-        lax.fori_loop(0, 2048 // Y_ROWS, last, 0)
+        lax.fori_loop(0, 2048 // Y_ROWS, body, 0)
 
     def out_copy(b, i):
         part = pl.ds(i * (Y_ROWS // 16), Y_ROWS // 16)
         return pltpu.make_async_copy(yo.at[b, part], y_ref.at[part, :, :, pl.ds(b * LANE, LANE)], out_sem.at[b, i])
 
     other_core = 1 - core
-    for h in range(2):
-        for pp in range(2):
-            arrived(me, other_core, h, pp)
-            stage1(me, h, pp, True)
-    for h in range(2):
-        for pp in range(2):
-            relay(h, pp)
-            arrived(x_slot, other_core, h, pp)
-            stage1(x_slot, h, pp, False)
-            arrived(y_slot, other_core, h, pp)
-            stage1(y_slot, h, pp, True)
-        stage23(OWN, h, h == 0, False)
-    for h in range(2):
-        relay_diag(h)
-        for pp in range(2):
-            arrived(d_slot, other_core, h, pp)
-            stage1(d_slot, h, pp, False)
-        stage23(OTHER, h, False, h == 1)
-
+
+    def own_chunk(h, _):
+        for pp in range(2):
+            arrived(OWN, OWN, other_core, h, pp)
+        for pp in range(2):
+            stage1(OWN, OWN, h, pp, True)
+        return 0
+
+    lax.fori_loop(0, 2, own_chunk, 0)
+
+    def direct_unit(s, _):
+        h, pp = s // 2, s % 2
+        relay(h, pp)
+        arrived(OWN, OTHER, other_core, h, pp)
+        arrived(OTHER, OWN, other_core, h, pp)
+        stage1(OWN, OTHER, h, pp, False)
+        stage1(OTHER, OWN, h, pp, True)
+
+        @pl.when(pp == 1)
+        def _():
+            stage2(OWN, h)
+            stage3(OWN, h, lambda: pl.when(h == 1)(lambda: relay_diag(0)))
+
+        return 0
+
+    lax.fori_loop(0, 4, direct_unit, 0)
+
+    def diagonal(h):
+        for pp in range(2):
+            arrived(OTHER, OTHER, other_core, h, pp)
+        for pp in range(2):
+            stage1(OTHER, OTHER, h, pp, False)
+        stage2(OTHER, h)
+
+    diagonal(0)
+    stage3(OTHER, 0, lambda: relay_diag(1))
+    diagonal(1)
+    stage3(OTHER, 1, final=True)
     for i in range(2048 // Y_ROWS):
         for b in range(2):
             out_copy(b, i).wait()
-    for cp in sends:
-        cp.wait_send()
+    for kind in range(7):
+        for h in range(2):
+            for pp in range(2):
+                send(kind, h, pp).wait_send()
 
 
 def solution(mesh):
@@ -256,7 +270,7 @@
                 pltpu.SemaphoreType.DMA((2, 16)),
                 pltpu.SemaphoreType.DMA((20,)),
                 pltpu.SemaphoreType.DMA((2, 2048 // Y_ROWS)),
-                pltpu.SemaphoreType.DMA((28,)),
+                pltpu.SemaphoreType.DMA((7, 2, 2)),
                 pltpu.SemaphoreType.DMA((2, 2, 2, 2, 2)),
             ],
             compiler_params=pltpu.CompilerParams(collective_id=0, has_side_effects=True, vmem_limit_bytes=62 * 2**20),

time: 101 us -> 96.9 us (0.959)
  Pallas kernels: 96.6 us -> 93.3 us
    pallas_call x1, Pallas kernels: 96.6 us -> 93.3 us  [local_apply(): pl.pallas_call(kernel, out_shape=jax.ShapeDtypeStruct((128, 4, 4, 256), F...]
where the time goes in v2:
time: 96.9 us; the launch traced here: 96.7 us
  Pallas kernels  93.3 us (96%)
  local copies, waits for them, and re-layouts  3.33 us (3%)
    pallas_call x1, Pallas kernels, local_apply(): pl.pallas_call(kernel, out_shape=jax.ShapeDtypeStruct((128, 4, 4, 256), F...  93.3 us
    unnamed x1, local copies, waits for them, and re-layouts  3.33 us

profile of v2, /device:TPU:0, one launch (start us, length us, event | category | flops | bytes accessed | tf_op | source)
XLA Modules:
  0.0 96.7 jit_solution(8444635917796305665)
XLA Ops:
  0.0 93.3 %two_site.1 = f32[128,4,4,256]{3,2,1,0:T(4,128)} custom-call(f32[128,4,4,256]{3,2,1,0:T(4,128)} %x_ref.1, f32[128,4,512]{2,1,0:T(4,128)} %l_ref.1, f32[4,4,4,4]{3,2,1,0:T(4,128)} %w_ref.1, f32[256,4,512]{2,1,0:T(4,128)} %r_ref.1), custom_call_target="tpu_custom_call" | custom-call | tf_op jit(solution)/shard_map/two_site/pallas_call | solution.py:251
  93.3 3.3 %copy.6 = f32[128,4,4,256]{3,2,1,0:T(4,128)} copy(f32[128,4,4,256]{3,2,1,0:T(4,128)} %two_site.1) | data formatting | bytes 4194304

commit v3 on v2

v3 whole, which is shorter than its diff:
```python
import functools

import jax
import jax.numpy as jnp
from jax import lax
from jax.experimental import pallas as pl
from jax.experimental.pallas import tpu as pltpu
from jax.sharding import PartitionSpec as P

HI = lax.Precision.HIGHEST
F32 = jnp.float32
LANE = 128
HALF = 64
GROUPS = 8
OWN, OTHER = 0, 1


def dot(a, b):
    return jnp.dot(a, b, precision=HI, preferred_element_type=F32)


def kernel(x_ref, l_ref, w_ref, r_ref, y_ref, xg, ln, l2, rt, t1r, t1g, t3s, ys, yo, kron, wa, wb, scale, load_sem, env_sem, out_sem, send_sem, recv_sem):
    by = lax.axis_index('by')
    bx = lax.axis_index('bx')
    core = lax.rem(bx, 2)
    chip = bx // 2
    sib = {'by': by, 'bx': bx + 1 - 2 * core}
    xnb = {'by': by, 'bx': lax.rem(bx + 2, 4)}
    ynb = {'by': 1 - by, 'bx': bx}

    def load(h, pq):
        i = h * 16 + pq
        return pltpu.make_async_copy(
            x_ref.at[:, pq // 4, pq % 4, pl.ds(h * LANE, LANE)],
            t1r.at[7, pl.ds(i // 8 * LANE, LANE), pl.ds(i % 8 * LANE, LANE)], load_sem.at[h, pq])

    for h in range(2):
        for pq in range(16):
            load(h, pq).start()
    env = []
    for half in range(2):
        for k in range(2):
            c0 = ((chip + half) % 2 * 2 + k) * LANE
            env.append(pltpu.make_async_copy(
                l_ref.at[:, :, pl.ds(pl.multiple_of(c0, LANE), LANE)], ln.at[half, k], env_sem.at[half * 2 + k]))
    for half in range(2):
        for h in range(2):
            f0 = ((by + half) % 2 * 2 + h) * LANE
            for r in range(4):
                env.append(pltpu.make_async_copy(
                    r_ref.at[:, r, pl.ds(pl.multiple_of(f0, LANE), LANE)],
                    t1r.at[6, pl.ds(half * 256, 256), pl.ds((h * 4 + r) * LANE, LANE)],
                    env_sem.at[4 + (half * 2 + h) * 4 + r]))
    for cp in env:
        cp.start()

    barrier = pltpu.get_barrier_semaphore()
    for d in (sib, xnb, ynb):
        pl.semaphore_signal(barrier, inc=1, device_id=d, device_id_type=pl.DeviceIdType.MESH)
    pl.semaphore_wait(barrier, 3)

    def send(kind, g):
        fh, ch = ((0, 0), (0, 0), (0, 0), (0, 1), (1, 0), (1, 1), (1, 1), (0, 1), (1, 0))[kind]
        dh, dc = ((0, 1), (1, 0), (0, 0), (0, 1), (1, 0), (1, 1), (1, 1), (1, 1), (1, 1))[kind]
        to = (xnb, ynb, sib, sib, sib, sib, sib, ynb, xnb)[kind]
        part = pl.ds(*((0, 8), (0, 8), (0, 8), (0, 8), (0, 8), (0, 4), (4, 4), (0, 4), (4, 4))[kind])
        return pltpu.make_async_remote_copy(
            src_ref=xg.at[fh, g, ch, core, part],
            dst_ref=xg.at[dh, g, dc, core, part],
            send_sem=send_sem.at[kind, g],
            recv_sem=recv_sem.at[dh, g, dc, core, int(kind in (6, 8))],
            device_id=to, device_id_type=pl.DeviceIdType.MESH)

    def arrived(fh, ch, k, g, half=None):
        part = pl.ds(0, 8) if half is None else pl.ds(4 * half, 4)
        ref = xg.at[fh, g, ch, k, part]
        pltpu.make_async_copy(ref, ref, recv_sem.at[fh, g, ch, k, 0 if half is None else half]).wait()

    low = lax.broadcasted_iota(jnp.int32, (LANE, LANE), 1) < HALF

    def swap(v0, v1):
        m = low[:v0.shape[0]]
        return jnp.where(m, v0, pltpu.roll(v1, HALF, 1)), jnp.where(m, pltpu.roll(v0, HALF, 1), v1)

    def split(h):
        for n in range(8):
            v = []
            for pq in (2 * n, 2 * n + 1):
                i = h * 16 + pq
                load(h, pq).wait()
                v.append(t1r[7, i // 8 * LANE:(i // 8 + 1) * LANE, i % 8 * LANE:(i % 8 + 1) * LANE])
            xg[OWN, 2 * h, OWN, core, n], xg[OWN, 2 * h + 1, OWN, core, n] = swap(*v)

    for h in range(2):
        split(h)
        for g in (2 * h, 2 * h + 1):
            for kind in range(3):
                send(kind, g).start()

    def relay(g):
        arrived(OWN, OTHER, core, g)
        send(3, g).start()
        send(7, g).start()
        arrived(OTHER, OWN, core, g)
        send(4, g).start()
        send(8, g).start()

    def relay_diag(g):
        for half in range(2):
            arrived(OTHER, OTHER, core, g, half)
            send(5 + half, g).start()

    for cp in env[:4]:
        cp.wait()
    for half in range(2):
        for k in range(2):
            l2[half, :, k * LANE:(k + 1) * LANE] = ln[half, k].reshape(512, LANE)
    wa[...] = jnp.zeros_like(wa)
    wb[...] = jnp.zeros_like(wb)
    lane8 = lax.broadcasted_iota(jnp.int32, (8, LANE), 1)
    row8 = lax.broadcasted_iota(jnp.int32, (8, LANE), 0)
    lane16 = lax.broadcasted_iota(jnp.int32, (16, LANE), 1)
    row16 = lax.broadcasted_iota(jnp.int32, (16, LANE), 0)

    def fill(i, carry):
        va, vb = carry
        i0, i1, i2 = i // 16, i // 4 % 4, i % 4
        for i3 in range(4):
            val = w_ref[i0, i1, i2, i3]
            va = jnp.where((row8 == i1) & (lane8 == i0 * 16 + i2 * 4 + i3), val, va)
            vb = jnp.where((row16 == i3 * 4 + i1) & (lane16 == i0 * 4 + i2), val, vb)
        return va, vb

    va, vb = lax.fori_loop(0, 64, fill, (jnp.zeros((8, LANE), F32), jnp.zeros((16, LANE), F32)))
    top = jnp.max(jnp.max(jnp.abs(va), axis=1, keepdims=True), axis=0, keepdims=True)
    scale[...] = jnp.broadcast_to(top, scale.shape)
    wa[...] = va / scale[...]
    wb[...] = vb / jnp.broadcast_to(top, (16, LANE))

    row = lax.broadcasted_iota(jnp.int32, (256, LANE), 0)
    a_mat = jnp.zeros((256, LANE), F32)
    for s in range(4):
        a_mat = jnp.where(row // 4 % 4 == s, wa[s:s + 1, :], a_mat)
    c_mat = jnp.zeros((256, LANE), F32)
    for rt_ in range(16):
        c_mat = jnp.where((row // 64) * 4 + row % 4 == rt_, wb[rt_:rt_ + 1, :], c_mat)
    col = lax.broadcasted_iota(jnp.int32, (LANE, 256), 1)
    pick = lax.broadcasted_iota(jnp.int32, (LANE, 256), 0)
    total = jnp.zeros((256, 256), F32)
    for v in range(4):
        left = dot(a_mat, jnp.where(pick == col % 4 * 16 + col // 64 * 4 + v, 1.0, 0.0).astype(F32))
        right = dot(c_mat, jnp.where(pick == v * 4 + col // 16 % 4, 1.0, 0.0).astype(F32))
        total = total + left * right
    krow = lax.broadcasted_iota(jnp.int32, (256, 256), 0)
    kcol = lax.broadcasted_iota(jnp.int32, (256, 256), 1)
    kron[...] = jnp.where(krow // 16 % 4 == kcol // 4 % 4, total, 0.0)
    for cp in env[4:]:
        cp.wait()
    for fc in range(4):
        for r in range(4):
            t = t1r[6, fc // 2 * 256:(fc // 2 + 1) * 256, (fc % 2 * 4 + r) * LANE:(fc % 2 * 4 + r + 1) * LANE].T
            rt[fc * 2, r * HALF:(r + 1) * HALF, :] = t[:HALF]
            rt[fc * 2 + 1, r * HALF:(r + 1) * HALF, :] = t[HALF:]

    def stage1(fh, ch, g, first):
        xs = jnp.concatenate([
            jnp.concatenate([xg[fh, g, ch, k, n] for n in range(8)], axis=1) for k in range(2)], axis=0)
        t = dot(l2[ch], xs)
        if first:
            t1r[fh * 4 + g] = t
            return
        for n in range(8):
            lanes = slice(n * LANE, (n + 1) * LANE)
            for m in range(2):
                v = [t[ab * LANE:(ab + 1) * LANE, lanes] + t1r[fh * 4 + g, ab * LANE:(ab + 1) * LANE, lanes] for ab in (2 * m, 2 * m + 1)]
                for qb, w in enumerate(swap(*v)):
                    t1g[:, (2 * n + qb) * 16:(2 * n + qb + 1) * 16, m * LANE:(m + 1) * LANE] = w.reshape(GROUPS, 16, LANE)

    def stage2(g):
        sc = scale[0:1, 0:1]

        def body(_, c):
            for i in range(GROUPS):
                t = dot(kron[...], t1g[i] * sc) * sc
                for rp in range(2):
                    for m in range(2):
                        v = [t[r * HALF:(r + 1) * HALF, m * LANE:(m + 1) * LANE] for r in (2 * rp, 2 * rp + 1)]
                        for n, w in enumerate(swap(*v)):
                            row0 = (2 * m + n) * 512 + i * 64
                            t3s[row0:row0 + 64, rp * LANE:(rp + 1) * LANE] = w
            return c

        lax.fori_loop(g, g + 1, body, 0)

    def stage3(fh, g, final=False):
        def body(_, c):
            part = dot(t3s[...], rt[fh * 4 + g])
            for b in range(2):
                v = part[:, b * LANE:(b + 1) * LANE]
                v = v + (jnp.where(g == 0, 0.0, ys[b]) if fh == 0 else ys[b])
                if final:
                    yo[b] = v.reshape(128, 4, 4, LANE)
                else:
                    ys[b] = v
            return c

        lax.fori_loop(g, g + 1, body, 0)

    other_core = 1 - core

    def own(i, _):
        for j in range(2):
            arrived(OWN, OWN, other_core, 2 * i + j)
        for j in range(2):
            stage1(OWN, OWN, 2 * i + j, True)
        return 0

    lax.fori_loop(0, 2, own, 0)

    def direct(g, _):
        relay(g)
        arrived(OWN, OTHER, other_core, g)
        arrived(OTHER, OWN, other_core, g)
        stage1(OWN, OTHER, g, False)
        stage1(OTHER, OWN, g, True)
        stage2(g)
        pl.when(g == 3)(lambda: relay_diag(0))
        stage3(OWN, g)
        return 0

    lax.fori_loop(0, 4, direct, 0)

    def diagonal(g, _):
        for half in range(2):
            arrived(OTHER, OTHER, other_core, g, half)
        stage1(OTHER, OTHER, g, False)
        stage2(g)
        pl.when(g < 3)(lambda: relay_diag(g + 1))
        pl.when(g < 3)(lambda: stage3(OTHER, g))
        pl.when(g == 3)(lambda: stage3(OTHER, g, True))
        return 0

    lax.fori_loop(0, 4, diagonal, 0)

    outs = [pltpu.make_async_copy(yo.at[b], y_ref.at[:, :, :, pl.ds(b * LANE, LANE)], out_sem.at[b]) for b in range(2)]
    for cp in outs:
        cp.start()
    for cp in outs:
        cp.wait()
    for kind in range(9):
        for g in range(4):
            send(kind, g).wait_send()


def solution(mesh):
    def local_apply(x, left, mpo, right):
        any_spec = pl.BlockSpec(memory_space=pl.ANY)
        return pl.pallas_call(
            kernel,
            out_shape=jax.ShapeDtypeStruct((128, 4, 4, 256), F32),
            in_specs=[any_spec, any_spec, pl.BlockSpec(memory_space=pltpu.SMEM), any_spec],
            out_specs=any_spec,
            scratch_shapes=[
                pltpu.VMEM((2, 4, 2, 2, 8, 128, LANE), F32),
                pltpu.VMEM((2, 2, 128, 4, LANE), F32),
                pltpu.VMEM((2, 512, 256), F32),
                pltpu.VMEM((8, 256, 256), F32),
                pltpu.VMEM((8, 512, 1024), F32),
                pltpu.VMEM((GROUPS, 256, 256), F32),
                pltpu.VMEM((2048, 256), F32),
                pltpu.VMEM((2, 2048, LANE), F32),
                pltpu.VMEM((2, 128, 4, 4, LANE), F32),
                pltpu.VMEM((256, 256), F32),
                pltpu.VMEM((8, LANE), F32),
                pltpu.VMEM((16, LANE), F32),
                pltpu.VMEM((8, LANE), F32),
                pltpu.SemaphoreType.DMA((2, 16)),
                pltpu.SemaphoreType.DMA((20,)),
                pltpu.SemaphoreType.DMA((2,)),
                pltpu.SemaphoreType.DMA((9, 4)),
                pltpu.SemaphoreType.DMA((2, 4, 2, 2, 2)),
            ],
            compiler_params=pltpu.CompilerParams(collective_id=0, has_side_effects=True, vmem_limit_bytes=62 * 2**20),
            name='two_site',
        )(x, left, mpo, right)

    return jax.shard_map(local_apply, mesh=mesh, in_specs=(P('bx', None, None, 'by'), P('bx', None, None), P(), P('by', None, None)), out_specs=P('bx', None, None, 'by'), check_vma=False)
```

time: 96.9 us -> 94.3 us (0.973)
  Pallas kernels: 93.3 us -> 90.8 us
    pallas_call x1, Pallas kernels: 93.3 us -> 90.8 us  [local_apply(): pl.pallas_call(kernel, out_shape=jax.ShapeDtypeStruct((128, 4, 4, 256), F...]
where the time goes in v3:
time: 94.3 us; the launch traced here: 94.1 us
  Pallas kernels  90.8 us (96%)
  local copies, waits for them, and re-layouts  3.33 us (4%)
    pallas_call x1, Pallas kernels, local_apply(): pl.pallas_call(kernel, out_shape=jax.ShapeDtypeStruct((128, 4, 4, 256), F...  90.8 us
    unnamed x1, local copies, waits for them, and re-layouts  3.33 us

profile of v3, /device:TPU:0, one launch (start us, length us, event | category | flops | bytes accessed | tf_op | source)
XLA Modules:
  0.0 94.1 jit_solution(1962396871809526851)
XLA Ops:
  0.0 90.8 %two_site.1 = f32[128,4,4,256]{3,2,1,0:T(4,128)} custom-call(f32[128,4,4,256]{3,2,1,0:T(4,128)} %x_ref.1, f32[128,4,512]{2,1,0:T(4,128)} %l_ref.1, f32[4,4,4,4]{3,2,1,0:T(4,128)} %w_ref.1, f32[256,4,512]{2,1,0:T(4,128)} %r_ref.1), custom_call_target="tpu_custom_call" | custom-call | tf_op jit(solution)/shard_map/two_site/pallas_call | solution.py:258
  90.8 3.3 %copy.6 = f32[128,4,4,256]{3,2,1,0:T(4,128)} copy(f32[128,4,4,256]{3,2,1,0:T(4,128)} %two_site.1) | data formatting | bytes 4194304

commit v4 on v3

--- a/solution.py
+++ b/solution.py
@@ -19,7 +19,7 @@
     return jnp.dot(a, b, precision=HI, preferred_element_type=F32)
 
 
-def kernel(x_ref, l_ref, w_ref, r_ref, y_ref, xg, ln, l2, rt, t1r, t1g, t3s, ys, yo, kron, wa, wb, scale, load_sem, env_sem, out_sem, send_sem, recv_sem):
+def kernel(x_ref, l_ref, w_hbm, r_ref, y_ref, xg, ln, l2, rt, t1r, t1g, t3s, ys, yo, kron, w_ref, wa, wb, scale, load_sem, env_sem, out_sem, send_sem, recv_sem):
     by = lax.axis_index('by')
     bx = lax.axis_index('bx')
     core = lax.rem(bx, 2)
@@ -32,7 +32,7 @@
         i = h * 16 + pq
         return pltpu.make_async_copy(
             x_ref.at[:, pq // 4, pq % 4, pl.ds(h * LANE, LANE)],
-            t1r.at[7, pl.ds(i // 8 * LANE, LANE), pl.ds(i % 8 * LANE, LANE)], load_sem.at[h, pq])
+            t1r.at[4, pl.ds(i // 8 * LANE, LANE), pl.ds(i % 8 * LANE, LANE)], load_sem.at[h, pq])
 
     for h in range(2):
         for pq in range(16):
@@ -49,8 +49,9 @@
             for r in range(4):
                 env.append(pltpu.make_async_copy(
                     r_ref.at[:, r, pl.ds(pl.multiple_of(f0, LANE), LANE)],
-                    t1r.at[6, pl.ds(half * 256, 256), pl.ds((h * 4 + r) * LANE, LANE)],
+                    t1r.at[3, pl.ds(half * 256, 256), pl.ds((h * 4 + r) * LANE, LANE)],
                     env_sem.at[4 + (half * 2 + h) * 4 + r]))
+    env.append(pltpu.make_async_copy(w_hbm, w_ref, env_sem.at[20]))
     for cp in env:
         cp.start()
 
@@ -83,19 +84,20 @@
         return jnp.where(m, v0, pltpu.roll(v1, HALF, 1)), jnp.where(m, pltpu.roll(v0, HALF, 1), v1)
 
     def split(h):
+        for pq in range(16):
+            load(h, pq).wait()
         for n in range(8):
-            v = []
-            for pq in (2 * n, 2 * n + 1):
-                i = h * 16 + pq
-                load(h, pq).wait()
-                v.append(t1r[7, i // 8 * LANE:(i // 8 + 1) * LANE, i % 8 * LANE:(i % 8 + 1) * LANE])
+            blocks = [(h * 16 + pq) for pq in (2 * n, 2 * n + 1)]
+            v = [t1r[4, i // 8 * LANE:(i // 8 + 1) * LANE, i % 8 * LANE:(i % 8 + 1) * LANE] for i in blocks]
             xg[OWN, 2 * h, OWN, core, n], xg[OWN, 2 * h + 1, OWN, core, n] = swap(*v)
 
-    for h in range(2):
-        split(h)
-        for g in (2 * h, 2 * h + 1):
-            for kind in range(3):
-                send(kind, g).start()
+    split(0)
+    for g in range(2):
+        for kind in range(3):
+            send(kind, g).start()
+    split(1)
+    for g in range(2, 4):
+        send(2, g).start()
 
     def relay(g):
         arrived(OWN, OTHER, core, g)
@@ -105,12 +107,17 @@
         send(4, g).start()
         send(8, g).start()
 
+        @pl.when(g < 2)
+        def _():
+            send(0, g + 2).start()
+            send(1, g + 2).start()
+
     def relay_diag(g):
         for half in range(2):
             arrived(OTHER, OTHER, core, g, half)
             send(5 + half, g).start()
 
-    for cp in env[:4]:
+    for cp in env[:4] + env[20:]:
         cp.wait()
     for half in range(2):
         for k in range(2):
@@ -131,7 +138,7 @@
             vb = jnp.where((row16 == i3 * 4 + i1) & (lane16 == i0 * 4 + i2), val, vb)
         return va, vb
 
-    va, vb = lax.fori_loop(0, 64, fill, (jnp.zeros((8, LANE), F32), jnp.zeros((16, LANE), F32)))
+    va, vb = lax.fori_loop(0, 64, fill, (jnp.zeros((8, LANE), F32), jnp.zeros((16, LANE), F32)), unroll=4)
     top = jnp.max(jnp.max(jnp.abs(va), axis=1, keepdims=True), axis=0, keepdims=True)
     scale[...] = jnp.broadcast_to(top, scale.shape)
     wa[...] = va / scale[...]
@@ -154,11 +161,11 @@
     krow = lax.broadcasted_iota(jnp.int32, (256, 256), 0)
     kcol = lax.broadcasted_iota(jnp.int32, (256, 256), 1)
     kron[...] = jnp.where(krow // 16 % 4 == kcol // 4 % 4, total, 0.0)
-    for cp in env[4:]:
+    for cp in env[4:20]:
         cp.wait()
     for fc in range(4):
         for r in range(4):
-            t = t1r[6, fc // 2 * 256:(fc // 2 + 1) * 256, (fc % 2 * 4 + r) * LANE:(fc % 2 * 4 + r + 1) * LANE].T
+            t = t1r[3, fc // 2 * 256:(fc // 2 + 1) * 256, (fc % 2 * 4 + r) * LANE:(fc % 2 * 4 + r + 1) * LANE].T
             rt[fc * 2, r * HALF:(r + 1) * HALF, :] = t[:HALF]
             rt[fc * 2 + 1, r * HALF:(r + 1) * HALF, :] = t[HALF:]
 
@@ -166,22 +173,23 @@
         xs = jnp.concatenate([
             jnp.concatenate([xg[fh, g, ch, k, n] for n in range(8)], axis=1) for k in range(2)], axis=0)
         t = dot(l2[ch], xs)
+        buf = g if fh == 0 else lax.rem(g + 4, 5)
         if first:
-            t1r[fh * 4 + g] = t
+            t1r[buf] = t
             return
         for n in range(8):
             lanes = slice(n * LANE, (n + 1) * LANE)
             for m in range(2):
-                v = [t[ab * LANE:(ab + 1) * LANE, lanes] + t1r[fh * 4 + g, ab * LANE:(ab + 1) * LANE, lanes] for ab in (2 * m, 2 * m + 1)]
+                v = [t[ab * LANE:(ab + 1) * LANE, lanes] + t1r[buf, ab * LANE:(ab + 1) * LANE, lanes] for ab in (2 * m, 2 * m + 1)]
                 for qb, w in enumerate(swap(*v)):
-                    t1g[:, (2 * n + qb) * 16:(2 * n + qb + 1) * 16, m * LANE:(m + 1) * LANE] = w.reshape(GROUPS, 16, LANE)
+                    t1g[:, (2 * n + qb) * 16:(2 * n + qb + 1) * 16, m * LANE:(m + 1) * LANE] = (w * scale[0:1, 0:1]).reshape(GROUPS, 16, LANE)
 
     def stage2(g):
         sc = scale[0:1, 0:1]
 
         def body(_, c):
             for i in range(GROUPS):
-                t = dot(kron[...], t1g[i] * sc) * sc
+                t = dot(kron[...], t1g[i]) * sc
                 for rp in range(2):
                     for m in range(2):
                         v = [t[r * HALF:(r + 1) * HALF, m * LANE:(m + 1) * LANE] for r in (2 * rp, 2 * rp + 1)]
@@ -217,6 +225,12 @@
 
     lax.fori_loop(0, 2, own, 0)
 
+    def diagonal(g):
+        for half in range(2):
+            arrived(OTHER, OTHER, other_core, g, half)
+        stage1(OTHER, OTHER, g, False)
+        stage2(g)
+
     def direct(g, _):
         relay(g)
         arrived(OWN, OTHER, other_core, g)
@@ -224,23 +238,25 @@
         stage1(OWN, OTHER, g, False)
         stage1(OTHER, OWN, g, True)
         stage2(g)
-        pl.when(g == 3)(lambda: relay_diag(0))
+        pl.when(g > 0)(lambda: relay_diag(g - 1))
         stage3(OWN, g)
+
+        @pl.when(g > 0)
+        def _():
+            diagonal(g - 1)
+            pl.when(g == 3)(lambda: relay_diag(g))
+            stage3(OTHER, g - 1)
+
         return 0
 
     lax.fori_loop(0, 4, direct, 0)
 
-    def diagonal(g, _):
-        for half in range(2):
-            arrived(OTHER, OTHER, other_core, g, half)
-        stage1(OTHER, OTHER, g, False)
-        stage2(g)
-        pl.when(g < 3)(lambda: relay_diag(g + 1))
-        pl.when(g < 3)(lambda: stage3(OTHER, g))
-        pl.when(g == 3)(lambda: stage3(OTHER, g, True))
+    def rest(g, _):
+        diagonal(g)
+        stage3(OTHER, g, True)
         return 0
 
-    lax.fori_loop(0, 4, diagonal, 0)
+    lax.fori_loop(3, 4, rest, 0)
 
     outs = [pltpu.make_async_copy(yo.at[b], y_ref.at[:, :, :, pl.ds(b * LANE, LANE)], out_sem.at[b]) for b in range(2)]
     for cp in outs:
@@ -258,24 +274,25 @@
         return pl.pallas_call(
             kernel,
             out_shape=jax.ShapeDtypeStruct((128, 4, 4, 256), F32),
-            in_specs=[any_spec, any_spec, pl.BlockSpec(memory_space=pltpu.SMEM), any_spec],
+            in_specs=[any_spec] * 4,
             out_specs=any_spec,
             scratch_shapes=[
                 pltpu.VMEM((2, 4, 2, 2, 8, 128, LANE), F32),
                 pltpu.VMEM((2, 2, 128, 4, LANE), F32),
                 pltpu.VMEM((2, 512, 256), F32),
                 pltpu.VMEM((8, 256, 256), F32),
-                pltpu.VMEM((8, 512, 1024), F32),
+                pltpu.VMEM((5, 512, 1024), F32),
                 pltpu.VMEM((GROUPS, 256, 256), F32),
                 pltpu.VMEM((2048, 256), F32),
                 pltpu.VMEM((2, 2048, LANE), F32),
                 pltpu.VMEM((2, 128, 4, 4, LANE), F32),
                 pltpu.VMEM((256, 256), F32),
+                pltpu.SMEM((4, 4, 4, 4), F32),
                 pltpu.VMEM((8, LANE), F32),
                 pltpu.VMEM((16, LANE), F32),
                 pltpu.VMEM((8, LANE), F32),
                 pltpu.SemaphoreType.DMA((2, 16)),
-                pltpu.SemaphoreType.DMA((20,)),
+                pltpu.SemaphoreType.DMA((21,)),
                 pltpu.SemaphoreType.DMA((2,)),
                 pltpu.SemaphoreType.DMA((9, 4)),
                 pltpu.SemaphoreType.DMA((2, 4, 2, 2, 2)),

time: 94.3 us -> 91 us (0.965)
  Pallas kernels: 90.8 us -> 87.6 us
    pallas_call x1, Pallas kernels: 90.8 us -> 87.6 us  [local_apply(): pl.pallas_call(kernel, out_shape=jax.ShapeDtypeStruct((128, 4, 4, 256), F...]
where the time goes in v4:
time: 91 us; the launch traced here: 90.9 us
  Pallas kernels  87.6 us (96%)
  local copies, waits for them, and re-layouts  3.33 us (4%)
    pallas_call x1, Pallas kernels, local_apply(): pl.pallas_call(kernel, out_shape=jax.ShapeDtypeStruct((128, 4, 4, 256), F...  87.6 us
    unnamed x1, local copies, waits for them, and re-layouts  3.33 us

profile of v4, /device:TPU:0, one launch (start us, length us, event | category | flops | bytes accessed | tf_op | source)
XLA Modules:
  0.0 90.9 jit_solution(2815467816084298020)
XLA Ops:
  0.0 87.6 %two_site.1 = f32[128,4,4,256]{3,2,1,0:T(4,128)} custom-call(f32[128,4,4,256]{3,2,1,0:T(4,128)} %x_ref.1, f32[128,4,512]{2,1,0:T(4,128)} %l_ref.1, f32[4,4,4,4]{3,2,1,0:T(4,128)} %w_hbm.1, f32[256,4,512]{2,1,0:T(4,128)} %r_ref.1), custom_call_target="tpu_custom_call" | custom-call | tf_op jit(solution)/shard_map/two_site/pallas_call | solution.py:274
  87.6 3.3 %copy.6 = f32[128,4,4,256]{3,2,1,0:T(4,128)} copy(f32[128,4,4,256]{3,2,1,0:T(4,128)} %two_site.1) | data formatting | bytes 4194304

commit v5 on v4

--- a/solution.py
+++ b/solution.py
@@ -37,6 +37,45 @@
     for h in range(2):
         for pq in range(16):
             load(h, pq).start()
+    barrier = pltpu.get_barrier_semaphore()
+    for d in (sib, xnb, ynb):
+        pl.semaphore_signal(barrier, inc=1, device_id=d, device_id_type=pl.DeviceIdType.MESH)
+    def send(kind, g):
+        fh, ch = ((0, 0), (0, 0), (0, 0), (0, 1), (1, 0), (1, 1), (1, 1), (0, 1), (1, 0))[kind]
+        dh, dc = ((0, 1), (1, 0), (0, 0), (0, 1), (1, 0), (1, 1), (1, 1), (1, 1), (1, 1))[kind]
+        to = (xnb, ynb, sib, sib, sib, sib, sib, ynb, xnb)[kind]
+        part = pl.ds(*((0, 8), (0, 8), (0, 8), (0, 8), (0, 8), (0, 4), (4, 4), (0, 4), (4, 4))[kind])
+        return pltpu.make_async_remote_copy(
+            src_ref=xg.at[fh, g, ch, core, part],
+            dst_ref=xg.at[dh, g, dc, core, part],
+            send_sem=send_sem.at[kind, g],
+            recv_sem=recv_sem.at[dh, g, dc, core, int(kind in (6, 8))],
+            device_id=to, device_id_type=pl.DeviceIdType.MESH)
+
+    def arrived(fh, ch, k, g, half=None):
+        part = pl.ds(0, 8) if half is None else pl.ds(4 * half, 4)
+        ref = xg.at[fh, g, ch, k, part]
+        pltpu.make_async_copy(ref, ref, recv_sem.at[fh, g, ch, k, 0 if half is None else half]).wait()
+
+    low = lax.broadcasted_iota(jnp.int32, (LANE, LANE), 1) < HALF
+
+    def swap(v0, v1):
+        m = low[:v0.shape[0]]
+        return jnp.where(m, v0, pltpu.roll(v1, HALF, 1)), jnp.where(m, pltpu.roll(v0, HALF, 1), v1)
+
+    def split(h):
+        for pq in range(16):
+            load(h, pq).wait()
+        for n in range(8):
+            blocks = [(h * 16 + pq) for pq in (2 * n, 2 * n + 1)]
+            v = [t1r[4, i // 8 * LANE:(i // 8 + 1) * LANE, i % 8 * LANE:(i % 8 + 1) * LANE] for i in blocks]
+            xg[OWN, 2 * h, OWN, core, n], xg[OWN, 2 * h + 1, OWN, core, n] = swap(*v)
+
+    split(0)
+    pl.semaphore_wait(barrier, 3)
+    for g in range(2):
+        for kind in range(3):
+            send(kind, g).start()
     env = []
     for half in range(2):
         for k in range(2):
@@ -55,46 +94,7 @@
     for cp in env:
         cp.start()
 
-    barrier = pltpu.get_barrier_semaphore()
-    for d in (sib, xnb, ynb):
-        pl.semaphore_signal(barrier, inc=1, device_id=d, device_id_type=pl.DeviceIdType.MESH)
-    pl.semaphore_wait(barrier, 3)
-
-    def send(kind, g):
-        fh, ch = ((0, 0), (0, 0), (0, 0), (0, 1), (1, 0), (1, 1), (1, 1), (0, 1), (1, 0))[kind]
-        dh, dc = ((0, 1), (1, 0), (0, 0), (0, 1), (1, 0), (1, 1), (1, 1), (1, 1), (1, 1))[kind]
-        to = (xnb, ynb, sib, sib, sib, sib, sib, ynb, xnb)[kind]
-        part = pl.ds(*((0, 8), (0, 8), (0, 8), (0, 8), (0, 8), (0, 4), (4, 4), (0, 4), (4, 4))[kind])
-        return pltpu.make_async_remote_copy(
-            src_ref=xg.at[fh, g, ch, core, part],
-            dst_ref=xg.at[dh, g, dc, core, part],
-            send_sem=send_sem.at[kind, g],
-            recv_sem=recv_sem.at[dh, g, dc, core, int(kind in (6, 8))],
-            device_id=to, device_id_type=pl.DeviceIdType.MESH)
-
-    def arrived(fh, ch, k, g, half=None):
-        part = pl.ds(0, 8) if half is None else pl.ds(4 * half, 4)
-        ref = xg.at[fh, g, ch, k, part]
-        pltpu.make_async_copy(ref, ref, recv_sem.at[fh, g, ch, k, 0 if half is None else half]).wait()
-
-    low = lax.broadcasted_iota(jnp.int32, (LANE, LANE), 1) < HALF
-
-    def swap(v0, v1):
-        m = low[:v0.shape[0]]
-        return jnp.where(m, v0, pltpu.roll(v1, HALF, 1)), jnp.where(m, pltpu.roll(v0, HALF, 1), v1)
-
-    def split(h):
-        for pq in range(16):
-            load(h, pq).wait()
-        for n in range(8):
-            blocks = [(h * 16 + pq) for pq in (2 * n, 2 * n + 1)]
-            v = [t1r[4, i // 8 * LANE:(i // 8 + 1) * LANE, i % 8 * LANE:(i % 8 + 1) * LANE] for i in blocks]
-            xg[OWN, 2 * h, OWN, core, n], xg[OWN, 2 * h + 1, OWN, core, n] = swap(*v)
-
-    split(0)
-    for g in range(2):
-        for kind in range(3):
-            send(kind, g).start()
+
     split(1)
     for g in range(2, 4):
         send(2, g).start()
@@ -201,18 +201,27 @@
         lax.fori_loop(g, g + 1, body, 0)
 
     def stage3(fh, g, final=False):
-        def body(_, c):
-            part = dot(t3s[...], rt[fh * 4 + g])
+        def body(i, c):
+            rows = pl.ds(i * 1024, 1024) if final else pl.ds(0, 2048)
+            part = dot(t3s[rows, :], rt[fh * 4 + g])
             for b in range(2):
                 v = part[:, b * LANE:(b + 1) * LANE]
-                v = v + (jnp.where(g == 0, 0.0, ys[b]) if fh == 0 else ys[b])
+                v = v + (jnp.where(g == 0, 0.0, ys[b, rows]) if fh == 0 else ys[b, rows])
                 if final:
-                    yo[b] = v.reshape(128, 4, 4, LANE)
+                    yo[b, pl.ds(i * 64, 64)] = v.reshape(64, 4, 4, LANE)
+                    out_copy(b, i).start()
                 else:
                     ys[b] = v
             return c
 
-        lax.fori_loop(g, g + 1, body, 0)
+        if final:
+            lax.fori_loop(0, 2, body, 0)
+        else:
+            lax.fori_loop(g, g + 1, body, 0)
+
+    def out_copy(b, i):
+        part = pl.ds(i * 64, 64)
+        return pltpu.make_async_copy(yo.at[b, part], y_ref.at[part, :, :, pl.ds(b * LANE, LANE)], out_sem.at[b, i])
 
     other_core = 1 - core
 
@@ -258,14 +267,12 @@
 
     lax.fori_loop(3, 4, rest, 0)
 
-    outs = [pltpu.make_async_copy(yo.at[b], y_ref.at[:, :, :, pl.ds(b * LANE, LANE)], out_sem.at[b]) for b in range(2)]
-    for cp in outs:
-        cp.start()
-    for cp in outs:
-        cp.wait()
     for kind in range(9):
         for g in range(4):
             send(kind, g).wait_send()
+    for i in range(2):
+        for b in range(2):
+            out_copy(b, i).wait()
 
 
 def solution(mesh):
@@ -293,7 +300,7 @@
                 pltpu.VMEM((8, LANE), F32),
                 pltpu.SemaphoreType.DMA((2, 16)),
                 pltpu.SemaphoreType.DMA((21,)),
-                pltpu.SemaphoreType.DMA((2,)),
+                pltpu.SemaphoreType.DMA((2, 2)),
                 pltpu.SemaphoreType.DMA((9, 4)),
                 pltpu.SemaphoreType.DMA((2, 4, 2, 2, 2)),
             ],

time: 91 us -> 90.7 us (level)
  no operation moved by 1% of the time
where the time goes in v5:
time: 90.7 us; the launch traced here: 90.5 us
  Pallas kernels  87.1 us (96%)
  local copies, waits for them, and re-layouts  3.33 us (4%)
    pallas_call x1, Pallas kernels, local_apply(): pl.pallas_call(kernel, out_shape=jax.ShapeDtypeStruct((128, 4, 4, 256), F...  87.1 us
    unnamed x1, local copies, waits for them, and re-layouts  3.33 us

profile of v5, /device:TPU:0, one launch (start us, length us, event | category | flops | bytes accessed | tf_op | source)
XLA Modules:
  0.0 90.5 jit_solution(997735431407402371)
XLA Ops:
  0.0 87.1 %two_site.1 = f32[128,4,4,256]{3,2,1,0:T(4,128)} custom-call(f32[128,4,4,256]{3,2,1,0:T(4,128)} %x_ref.1, f32[128,4,512]{2,1,0:T(4,128)} %l_ref.1, f32[4,4,4,4]{3,2,1,0:T(4,128)} %w_hbm.1, f32[256,4,512]{2,1,0:T(4,128)} %r_ref.1), custom_call_target="tpu_custom_call" | custom-call | tf_op jit(solution)/shard_map/two_site/pallas_call | solution.py:281
  87.2 3.3 %copy.6 = f32[128,4,4,256]{3,2,1,0:T(4,128)} copy(f32[128,4,4,256]{3,2,1,0:T(4,128)} %two_site.1) | data formatting | bytes 4194304

commit v6 on v5

--- a/solution.py
+++ b/solution.py
@@ -40,22 +40,29 @@
     barrier = pltpu.get_barrier_semaphore()
     for d in (sib, xnb, ynb):
         pl.semaphore_signal(barrier, inc=1, device_id=d, device_id_type=pl.DeviceIdType.MESH)
-    def send(kind, g):
-        fh, ch = ((0, 0), (0, 0), (0, 0), (0, 1), (1, 0), (1, 1), (1, 1), (0, 1), (1, 0))[kind]
-        dh, dc = ((0, 1), (1, 0), (0, 0), (0, 1), (1, 0), (1, 1), (1, 1), (1, 1), (1, 1))[kind]
-        to = (xnb, ynb, sib, sib, sib, sib, sib, ynb, xnb)[kind]
-        part = pl.ds(*((0, 8), (0, 8), (0, 8), (0, 8), (0, 8), (0, 4), (4, 4), (0, 4), (4, 4))[kind])
+    def send(kind, g, half):
+        fh, ch = ((0, 0), (0, 0), (0, 0), (0, 1), (1, 0), (1, 1), (half, 1 - half))[kind]
+        dh, dc = ((0, 1), (1, 0), (0, 0), (0, 1), (1, 0), (1, 1), (1, 1))[kind]
+        to = (xnb, ynb, sib, sib, sib, sib, (ynb, xnb)[half])[kind]
         return pltpu.make_async_remote_copy(
-            src_ref=xg.at[fh, g, ch, core, part],
-            dst_ref=xg.at[dh, g, dc, core, part],
-            send_sem=send_sem.at[kind, g],
-            recv_sem=recv_sem.at[dh, g, dc, core, int(kind in (6, 8))],
+            src_ref=xg.at[fh, g, ch, core, pl.ds(4 * half, 4)],
+            dst_ref=xg.at[dh, g, dc, core, pl.ds(4 * half, 4)],
+            send_sem=send_sem.at[kind, g, half],
+            recv_sem=recv_sem.at[dh, g, dc, core, half],
             device_id=to, device_id_type=pl.DeviceIdType.MESH)
 
-    def arrived(fh, ch, k, g, half=None):
-        part = pl.ds(0, 8) if half is None else pl.ds(4 * half, 4)
-        ref = xg.at[fh, g, ch, k, part]
-        pltpu.make_async_copy(ref, ref, recv_sem.at[fh, g, ch, k, 0 if half is None else half]).wait()
+    def arrived(fh, ch, k, g, half):
+        ref = xg.at[fh, g, ch, k, pl.ds(4 * half, 4)]
+        pltpu.make_async_copy(ref, ref, recv_sem.at[fh, g, ch, k, half]).wait()
+
+    def all_arrived(fh, ch, g):
+        for half in range(2):
+            arrived(fh, ch, 1 - core, g, half)
+
+    def direct_sends(g):
+        for half in range(2):
+            send(0, g, half).start()
+            send(1, g, half).start()
 
     low = lax.broadcasted_iota(jnp.int32, (LANE, LANE), 1) < HALF
 
@@ -74,8 +81,10 @@
     split(0)
     pl.semaphore_wait(barrier, 3)
     for g in range(2):
-        for kind in range(3):
-            send(kind, g).start()
+        direct_sends(g)
+    for g in range(2):
+        for half in range(2):
+            send(2, g, half).start()
     env = []
     for half in range(2):
         for k in range(2):
@@ -97,25 +106,25 @@
 
     split(1)
     for g in range(2, 4):
-        send(2, g).start()
+        for half in range(2):
+            send(2, g, half).start()
 
     def relay(g):
-        arrived(OWN, OTHER, core, g)
-        send(3, g).start()
-        send(7, g).start()
-        arrived(OTHER, OWN, core, g)
-        send(4, g).start()
-        send(8, g).start()
-
-        @pl.when(g < 2)
-        def _():
-            send(0, g + 2).start()
-            send(1, g + 2).start()
+        for half in range(2):
+            arrived(OWN, OTHER, core, g, half)
+            send(3, g, half).start()
+            if half == 0:
+                send(6, g, half).start()
+            arrived(OTHER, OWN, core, g, half)
+            send(4, g, half).start()
+            if half == 1:
+                send(6, g, half).start()
+        pl.when(g < 2)(lambda: direct_sends(g + 2))
 
     def relay_diag(g):
         for half in range(2):
             arrived(OTHER, OTHER, core, g, half)
-            send(5 + half, g).start()
+            send(5, g, half).start()
 
     for cp in env[:4] + env[20:]:
         cp.wait()
@@ -223,11 +232,9 @@
         part = pl.ds(i * 64, 64)
         return pltpu.make_async_copy(yo.at[b, part], y_ref.at[part, :, :, pl.ds(b * LANE, LANE)], out_sem.at[b, i])
 
-    other_core = 1 - core
-
     def own(i, _):
         for j in range(2):
-            arrived(OWN, OWN, other_core, 2 * i + j)
+            all_arrived(OWN, OWN, 2 * i + j)
         for j in range(2):
             stage1(OWN, OWN, 2 * i + j, True)
         return 0
@@ -235,15 +242,14 @@
     lax.fori_loop(0, 2, own, 0)
 
     def diagonal(g):
-        for half in range(2):
-            arrived(OTHER, OTHER, other_core, g, half)
+        all_arrived(OTHER, OTHER, g)
         stage1(OTHER, OTHER, g, False)
         stage2(g)
 
     def direct(g, _):
         relay(g)
-        arrived(OWN, OTHER, other_core, g)
-        arrived(OTHER, OWN, other_core, g)
+        all_arrived(OWN, OTHER, g)
+        all_arrived(OTHER, OWN, g)
         stage1(OWN, OTHER, g, False)
         stage1(OTHER, OWN, g, True)
         stage2(g)
@@ -267,9 +273,10 @@
 
     lax.fori_loop(3, 4, rest, 0)
 
-    for kind in range(9):
+    for kind in range(7):
         for g in range(4):
-            send(kind, g).wait_send()
+            for half in range(2):
+                send(kind, g, half).wait_send()
     for i in range(2):
         for b in range(2):
             out_copy(b, i).wait()
@@ -301,7 +308,7 @@
                 pltpu.SemaphoreType.DMA((2, 16)),
                 pltpu.SemaphoreType.DMA((21,)),
                 pltpu.SemaphoreType.DMA((2, 2)),
-                pltpu.SemaphoreType.DMA((9, 4)),
+                pltpu.SemaphoreType.DMA((7, 4, 2)),
                 pltpu.SemaphoreType.DMA((2, 4, 2, 2, 2)),
             ],
             compiler_params=pltpu.CompilerParams(collective_id=0, has_side_effects=True, vmem_limit_bytes=62 * 2**20),

time: 90.7 us -> 90.1 us (level)
  no operation moved by 1% of the time
where the time goes in v6:
time: 90.1 us; the launch traced here: 89.9 us
  Pallas kernels  86.6 us (96%)
  local copies, waits for them, and re-layouts  3.33 us (4%)
    pallas_call x1, Pallas kernels, local_apply(): pl.pallas_call(kernel, out_shape=jax.ShapeDtypeStruct((128, 4, 4, 256), F...  86.6 us
    unnamed x1, local copies, waits for them, and re-layouts  3.33 us

profile of v6, /device:TPU:0, one launch (start us, length us, event | category | flops | bytes accessed | tf_op | source)
XLA Modules:
  0.0 89.9 jit_solution(1545415610102778229)
XLA Ops:
  0.0 86.6 %two_site.1 = f32[128,4,4,256]{3,2,1,0:T(4,128)} custom-call(f32[128,4,4,256]{3,2,1,0:T(4,128)} %x_ref.1, f32[128,4,512]{2,1,0:T(4,128)} %l_ref.1, f32[4,4,4,4]{3,2,1,0:T(4,128)} %w_hbm.1, f32[256,4,512]{2,1,0:T(4,128)} %r_ref.1), custom_call_target="tpu_custom_call" | custom-call | tf_op jit(solution)/shard_map/two_site/pallas_call | solution.py:288
  86.6 3.3 %copy.6 = f32[128,4,4,256]{3,2,1,0:T(4,128)} copy(f32[128,4,4,256]{3,2,1,0:T(4,128)} %two_site.1) | data formatting | bytes 4194304

commit v7 on v6

--- a/solution.py
+++ b/solution.py
@@ -19,7 +19,7 @@
     return jnp.dot(a, b, precision=HI, preferred_element_type=F32)
 
 
-def kernel(x_ref, l_ref, w_hbm, r_ref, y_ref, xg, ln, l2, rt, t1r, t1g, t3s, ys, yo, kron, w_ref, wa, wb, scale, load_sem, env_sem, out_sem, send_sem, recv_sem):
+def kernel(x_ref, l_ref, w_hbm, r_ref, y_ref, xg, ln, l2, rt, t1r, t1g, t3s, ys, yo, kron, w_ref, wa, wb, scale, load_sem, env_sem, out_sem, send_sem, recv_sem, dsend_sem, drecv_sem):
     by = lax.axis_index('by')
     bx = lax.axis_index('bx')
     core = lax.rem(bx, 2)
@@ -41,19 +41,34 @@
     for d in (sib, xnb, ynb):
         pl.semaphore_signal(barrier, inc=1, device_id=d, device_id_type=pl.DeviceIdType.MESH)
     def send(kind, g, half):
-        fh, ch = ((0, 0), (0, 0), (0, 0), (0, 1), (1, 0), (1, 1), (half, 1 - half))[kind]
-        dh, dc = ((0, 1), (1, 0), (0, 0), (0, 1), (1, 0), (1, 1), (1, 1))[kind]
-        to = (xnb, ynb, sib, sib, sib, sib, (ynb, xnb)[half])[kind]
+        fh, ch = ((0, 0), (0, 0), (0, 0), (0, 1), (1, 0))[kind]
+        dh, dc = ((0, 1), (1, 0), (0, 0), (0, 1), (1, 0))[kind]
         return pltpu.make_async_remote_copy(
             src_ref=xg.at[fh, g, ch, core, pl.ds(4 * half, 4)],
             dst_ref=xg.at[dh, g, dc, core, pl.ds(4 * half, 4)],
             send_sem=send_sem.at[kind, g, half],
             recv_sem=recv_sem.at[dh, g, dc, core, half],
-            device_id=to, device_id_type=pl.DeviceIdType.MESH)
+            device_id=(xnb, ynb, sib, sib, sib)[kind], device_id_type=pl.DeviceIdType.MESH)
+
+    def send_diag(kind, g, half, sub):
+        fh, ch = ((half, 1 - half), (1, 1))[kind]
+        part = pl.ds(4 * half + 2 * sub, 2)
+        over = {'by': lax.rem(by + 1 - half, 2), 'bx': lax.rem(bx + 2 * half, 4)}
+        return pltpu.make_async_remote_copy(
+            src_ref=xg.at[fh, g, ch, core, part],
+            dst_ref=xg.at[1, g, 1, core, part],
+            send_sem=dsend_sem.at[kind, g, half, sub],
+            recv_sem=drecv_sem.at[g, core, half, sub],
+            device_id=(over, sib)[kind], device_id_type=pl.DeviceIdType.MESH)
 
     def arrived(fh, ch, k, g, half):
         ref = xg.at[fh, g, ch, k, pl.ds(4 * half, 4)]
         pltpu.make_async_copy(ref, ref, recv_sem.at[fh, g, ch, k, half]).wait()
+
+    def arrived_diag(k, g, sub):
+        for half in range(2):
+            ref = xg.at[1, g, 1, k, pl.ds(4 * half + 2 * sub, 2)]
+            pltpu.make_async_copy(ref, ref, drecv_sem.at[g, k, half, sub]).wait()
 
     def all_arrived(fh, ch, g):
         for half in range(2):
@@ -109,22 +124,18 @@
         for half in range(2):
             send(2, g, half).start()
 
-    def relay(g):
-        for half in range(2):
-            arrived(OWN, OTHER, core, g, half)
-            send(3, g, half).start()
-            if half == 0:
-                send(6, g, half).start()
-            arrived(OTHER, OWN, core, g, half)
-            send(4, g, half).start()
-            if half == 1:
-                send(6, g, half).start()
-        pl.when(g < 2)(lambda: direct_sends(g + 2))
-
-    def relay_diag(g):
-        for half in range(2):
-            arrived(OTHER, OTHER, core, g, half)
-            send(5, g, half).start()
+    def relay(g, half):
+        arrived(OWN, OTHER, core, g, half)
+        send(3, g, half).start()
+        arrived(OTHER, OWN, core, g, half)
+        send(4, g, half).start()
+        for sub in range(2):
+            send_diag(0, g, half, sub).start()
+
+    def relay_diag(g, sub):
+        arrived_diag(core, g, sub)
+        for half in range(2):
+            send_diag(1, g, half, sub).start()
 
     for cp in env[:4] + env[20:]:
         cp.wait()
@@ -178,20 +189,23 @@
             rt[fc * 2, r * HALF:(r + 1) * HALF, :] = t[:HALF]
             rt[fc * 2 + 1, r * HALF:(r + 1) * HALF, :] = t[HALF:]
 
-    def stage1(fh, ch, g, first):
+    def stage1(fh, ch, g, first, pairs):
         xs = jnp.concatenate([
-            jnp.concatenate([xg[fh, g, ch, k, n] for n in range(8)], axis=1) for k in range(2)], axis=0)
+            jnp.concatenate([xg[fh, g, ch, k, n] for n in pairs], axis=1) for k in range(2)], axis=0)
         t = dot(l2[ch], xs)
         buf = g if fh == 0 else lax.rem(g + 4, 5)
-        if first:
-            t1r[buf] = t
-            return
-        for n in range(8):
-            lanes = slice(n * LANE, (n + 1) * LANE)
+        for i, n in enumerate(pairs):
+            lanes = slice(i * LANE, (i + 1) * LANE)
+            held = pl.ds(n * LANE if isinstance(n, int) else pl.multiple_of(n * LANE, LANE), LANE)
+            if first:
+                t1r[buf, :, held] = t[:, lanes]
+                continue
             for m in range(2):
-                v = [t[ab * LANE:(ab + 1) * LANE, lanes] + t1r[buf, ab * LANE:(ab + 1) * LANE, lanes] for ab in (2 * m, 2 * m + 1)]
+                v = [t[ab * LANE:(ab + 1) * LANE, lanes] + t1r[buf, ab * LANE:(ab + 1) * LANE, held] for ab in (2 * m, 2 * m + 1)]
                 for qb, w in enumerate(swap(*v)):
-                    t1g[:, (2 * n + qb) * 16:(2 * n + qb + 1) * 16, m * LANE:(m + 1) * LANE] = (w * scale[0:1, 0:1]).reshape(GROUPS, 16, LANE)
+                    row0 = (2 * n + qb) * 16
+                    row0 = row0 if isinstance(n, int) else pl.multiple_of(row0, 16)
+                    t1g[:, pl.ds(row0, 16), m * LANE:(m + 1) * LANE] = (w * scale[0:1, 0:1]).reshape(GROUPS, 16, LANE)
 
     def stage2(g):
         sc = scale[0:1, 0:1]
@@ -236,30 +250,38 @@
         for j in range(2):
             all_arrived(OWN, OWN, 2 * i + j)
         for j in range(2):
-            stage1(OWN, OWN, 2 * i + j, True)
+            stage1(OWN, OWN, 2 * i + j, True, range(8))
         return 0
 
     lax.fori_loop(0, 2, own, 0)
 
-    def diagonal(g):
-        all_arrived(OTHER, OTHER, g)
-        stage1(OTHER, OTHER, g, False)
+    def direct_half(g, half):
+        relay(g, half)
+        arrived(OWN, OTHER, 1 - core, g, half)
+        arrived(OTHER, OWN, 1 - core, g, half)
+        pairs = [4 * half + n for n in range(4)]
+        stage1(OWN, OTHER, g, False, pairs)
+        stage1(OTHER, OWN, g, True, pairs)
+
+    def direct(g, _):
+        lax.fori_loop(0, 2, lambda half, c: (direct_half(g, half), c)[1], 0)
+        pl.when(g < 2)(lambda: direct_sends(g + 2))
         stage2(g)
-
-    def direct(g, _):
-        relay(g)
-        all_arrived(OWN, OTHER, g)
-        all_arrived(OTHER, OWN, g)
-        stage1(OWN, OTHER, g, False)
-        stage1(OTHER, OWN, g, True)
-        stage2(g)
-        pl.when(g > 0)(lambda: relay_diag(g - 1))
-        stage3(OWN, g)
 
         @pl.when(g > 0)
         def _():
-            diagonal(g - 1)
-            pl.when(g == 3)(lambda: relay_diag(g))
+            for sub in range(2):
+                relay_diag(g - 1, sub)
+
+        stage3(OWN, g)
+
+        @pl.when(g > 0)
+        def _():
+            for sub in range(2):
+                arrived_diag(1 - core, g - 1, sub)
+            stage1(OTHER, OTHER, g - 1, False, range(8))
+            stage2(g - 1)
+            pl.when(g == 3)(lambda: relay_diag(g, 0))
             stage3(OTHER, g - 1)
 
         return 0
@@ -267,16 +289,23 @@
     lax.fori_loop(0, 4, direct, 0)
 
     def rest(g, _):
-        diagonal(g)
+        relay_diag(g, 1)
+        for sub in range(2):
+            arrived_diag(1 - core, g, sub)
+            stage1(OTHER, OTHER, g, False, [2 * sub, 2 * sub + 1, 2 * sub + 4, 2 * sub + 5])
+        stage2(g)
         stage3(OTHER, g, True)
         return 0
 
     lax.fori_loop(3, 4, rest, 0)
 
-    for kind in range(7):
-        for g in range(4):
-            for half in range(2):
+    for g in range(4):
+        for half in range(2):
+            for kind in range(5):
                 send(kind, g, half).wait_send()
+            for kind in range(2):
+                for sub in range(2):
+                    send_diag(kind, g, half, sub).wait_send()
     for i in range(2):
         for b in range(2):
             out_copy(b, i).wait()
@@ -308,8 +337,10 @@
                 pltpu.SemaphoreType.DMA((2, 16)),
                 pltpu.SemaphoreType.DMA((21,)),
                 pltpu.SemaphoreType.DMA((2, 2)),
-                pltpu.SemaphoreType.DMA((7, 4, 2)),
+                pltpu.SemaphoreType.DMA((5, 4, 2)),
                 pltpu.SemaphoreType.DMA((2, 4, 2, 2, 2)),
+                pltpu.SemaphoreType.DMA((2, 4, 2, 2)),
+                pltpu.SemaphoreType.DMA((4, 2, 2, 2)),
             ],
             compiler_params=pltpu.CompilerParams(collective_id=0, has_side_effects=True, vmem_limit_bytes=62 * 2**20),
             name='two_site',

time: 90.1 us -> 92.5 us (1.027)
  Pallas kernels: 86.6 us -> 89 us
    pallas_call x1, Pallas kernels: 86.6 us -> 89 us  [local_apply(): pl.pallas_call(kernel, out_shape=jax.ShapeDtypeStruct((128, 4, 4, 256), F...]
where the time goes in v7:
time: 92.5 us; the launch traced here: 92.3 us
  Pallas kernels  89 us (96%)
  local copies, waits for them, and re-layouts  3.33 us (4%)
    pallas_call x1, Pallas kernels, local_apply(): pl.pallas_call(kernel, out_shape=jax.ShapeDtypeStruct((128, 4, 4, 256), F...  89 us
    unnamed x1, local copies, waits for them, and re-layouts  3.33 us

profile of v7, /device:TPU:0, one launch (start us, length us, event | category | flops | bytes accessed | tf_op | source)
XLA Modules:
  0.0 92.3 jit_solution(9444253928537713396)
XLA Ops:
  0.0 89.0 %two_site.1 = f32[128,4,4,256]{3,2,1,0:T(4,128)} custom-call(f32[128,4,4,256]{3,2,1,0:T(4,128)} %x_ref.1, f32[128,4,512]{2,1,0:T(4,128)} %l_ref.1, f32[4,4,4,4]{3,2,1,0:T(4,128)} %w_hbm.1, f32[256,4,512]{2,1,0:T(4,128)} %r_ref.1), custom_call_target="tpu_custom_call" | custom-call | tf_op jit(solution)/shard_map/two_site/pallas_call | solution.py:317
  89.0 3.3 %copy.6 = f32[128,4,4,256]{3,2,1,0:T(4,128)} copy(f32[128,4,4,256]{3,2,1,0:T(4,128)} %two_site.1) | data formatting | bytes 4194304

commit v8 on v6

--- a/solution.py
+++ b/solution.py
@@ -40,27 +40,29 @@
     barrier = pltpu.get_barrier_semaphore()
     for d in (sib, xnb, ynb):
         pl.semaphore_signal(barrier, inc=1, device_id=d, device_id_type=pl.DeviceIdType.MESH)
-    def send(kind, g, half):
-        fh, ch = ((0, 0), (0, 0), (0, 0), (0, 1), (1, 0), (1, 1), (half, 1 - half))[kind]
+    def pairs(half):
+        return pl.ds(0, 8) if half is None else pl.ds(4 * half, 4)
+
+    def send(kind, g, half=None):
+        fh, ch = ((0, 0), (0, 0), (0, 0), (0, 1), (1, 0), (1, 1), (half, 1 - (half or 0)))[kind]
         dh, dc = ((0, 1), (1, 0), (0, 0), (0, 1), (1, 0), (1, 1), (1, 1))[kind]
-        to = (xnb, ynb, sib, sib, sib, sib, (ynb, xnb)[half])[kind]
+        to = (xnb, ynb, sib, sib, sib, sib, (ynb, xnb)[half or 0])[kind]
         return pltpu.make_async_remote_copy(
-            src_ref=xg.at[fh, g, ch, core, pl.ds(4 * half, 4)],
-            dst_ref=xg.at[dh, g, dc, core, pl.ds(4 * half, 4)],
-            send_sem=send_sem.at[kind, g, half],
-            recv_sem=recv_sem.at[dh, g, dc, core, half],
+            src_ref=xg.at[fh, g, ch, core, pairs(half)],
+            dst_ref=xg.at[dh, g, dc, core, pairs(half)],
+            send_sem=send_sem.at[kind, g, half or 0],
+            recv_sem=recv_sem.at[dh, g, dc, core, half or 0],
             device_id=to, device_id_type=pl.DeviceIdType.MESH)
 
-    def arrived(fh, ch, k, g, half):
-        ref = xg.at[fh, g, ch, k, pl.ds(4 * half, 4)]
-        pltpu.make_async_copy(ref, ref, recv_sem.at[fh, g, ch, k, half]).wait()
-
-    def all_arrived(fh, ch, g):
-        for half in range(2):
-            arrived(fh, ch, 1 - core, g, half)
+    def arrived(fh, ch, k, g, half=None):
+        ref = xg.at[fh, g, ch, k, pairs(half)]
+        pltpu.make_async_copy(ref, ref, recv_sem.at[fh, g, ch, k, half or 0]).wait()
+
+    def parts(g):
+        return (None,) if g < 3 else (0, 1)
 
     def direct_sends(g):
-        for half in range(2):
+        for half in parts(g):
             send(0, g, half).start()
             send(1, g, half).start()
 
@@ -83,8 +85,7 @@
     for g in range(2):
         direct_sends(g)
     for g in range(2):
-        for half in range(2):
-            send(2, g, half).start()
+        send(2, g).start()
     env = []
     for half in range(2):
         for k in range(2):
@@ -106,20 +107,36 @@
 
     split(1)
     for g in range(2, 4):
-        for half in range(2):
-            send(2, g, half).start()
+        send(2, g).start()
 
     def relay(g):
-        for half in range(2):
-            arrived(OWN, OTHER, core, g, half)
-            send(3, g, half).start()
-            if half == 0:
-                send(6, g, half).start()
-            arrived(OTHER, OWN, core, g, half)
-            send(4, g, half).start()
-            if half == 1:
-                send(6, g, half).start()
-        pl.when(g < 2)(lambda: direct_sends(g + 2))
+        @pl.when(g < 3)
+        def _():
+            arrived(OWN, OTHER, core, g)
+            send(3, g).start()
+            send(6, g, 0).start()
+            arrived(OTHER, OWN, core, g)
+            send(4, g).start()
+            send(6, g, 1).start()
+            pl.when(g == 0)(lambda: direct_sends(2))
+            pl.when(g == 1)(lambda: direct_sends(3))
+            arrived(OWN, OTHER, 1 - core, g)
+            arrived(OTHER, OWN, 1 - core, g)
+
+        @pl.when(g == 3)
+        def _():
+            for half in range(2):
+                arrived(OWN, OTHER, core, g, half)
+                send(3, g, half).start()
+                if half == 0:
+                    send(6, g, 0).start()
+                arrived(OTHER, OWN, core, g, half)
+                send(4, g, half).start()
+                if half == 1:
+                    send(6, g, 1).start()
+            for half in range(2):
+                arrived(OWN, OTHER, 1 - core, g, half)
+                arrived(OTHER, OWN, 1 - core, g, half)
 
     def relay_diag(g):
         for half in range(2):
@@ -234,7 +251,7 @@
 
     def own(i, _):
         for j in range(2):
-            all_arrived(OWN, OWN, 2 * i + j)
+            arrived(OWN, OWN, 1 - core, 2 * i + j)
         for j in range(2):
             stage1(OWN, OWN, 2 * i + j, True)
         return 0
@@ -242,14 +259,13 @@
     lax.fori_loop(0, 2, own, 0)
 
     def diagonal(g):
-        all_arrived(OTHER, OTHER, g)
+        for half in range(2):
+            arrived(OTHER, OTHER, 1 - core, g, half)
         stage1(OTHER, OTHER, g, False)
         stage2(g)
 
     def direct(g, _):
         relay(g)
-        all_arrived(OWN, OTHER, g)
-        all_arrived(OTHER, OWN, g)
         stage1(OWN, OTHER, g, False)
         stage1(OTHER, OWN, g, True)
         stage2(g)
@@ -273,9 +289,9 @@
 
     lax.fori_loop(3, 4, rest, 0)
 
-    for kind in range(7):
-        for g in range(4):
-            for half in range(2):
+    for g in range(4):
+        for kind in range(7):
+            for half in ((None,) if kind == 2 else (0, 1) if kind > 4 else parts(g)):
                 send(kind, g, half).wait_send()
     for i in range(2):
         for b in range(2):

time: 90.1 us -> 90.1 us (level)
  no operation moved by 1% of the time
where the time goes in v8:
time: 90.1 us; the launch traced here: 89.9 us
  Pallas kernels  86.6 us (96%)
  local copies, waits for them, and re-layouts  3.33 us (4%)
    pallas_call x1, Pallas kernels, local_apply(): pl.pallas_call(kernel, out_shape=jax.ShapeDtypeStruct((128, 4, 4, 256), F...  86.6 us
    unnamed x1, local copies, waits for them, and re-layouts  3.33 us

profile of v8, /device:TPU:0, one launch (start us, length us, event | category | flops | bytes accessed | tf_op | source)
XLA Modules:
  0.0 89.9 jit_solution(17975080506455307173)
XLA Ops:
  0.0 86.6 %two_site.1 = f32[128,4,4,256]{3,2,1,0:T(4,128)} custom-call(f32[128,4,4,256]{3,2,1,0:T(4,128)} %x_ref.1, f32[128,4,512]{2,1,0:T(4,128)} %l_ref.1, f32[4,4,4,4]{3,2,1,0:T(4,128)} %w_hbm.1, f32[256,4,512]{2,1,0:T(4,128)} %r_ref.1), custom_call_target="tpu_custom_call" | custom-call | tf_op jit(solution)/shard_map/two_site/pallas_call | solution.py:304
  86.6 3.3 %copy.6 = f32[128,4,4,256]{3,2,1,0:T(4,128)} copy(f32[128,4,4,256]{3,2,1,0:T(4,128)} %two_site.1) | data formatting | bytes 4194304

commit v9 on v8

--- a/solution.py
+++ b/solution.py
@@ -44,19 +44,20 @@
         return pl.ds(0, 8) if half is None else pl.ds(4 * half, 4)
 
     def send(kind, g, half=None):
-        fh, ch = ((0, 0), (0, 0), (0, 0), (0, 1), (1, 0), (1, 1), (half, 1 - (half or 0)))[kind]
+        h0 = 0 if half is None else half
+        fh, ch = ((0, 0), (0, 0), (0, 0), (0, 1), (1, 0), (1, 1), (h0, 1 - h0))[kind]
         dh, dc = ((0, 1), (1, 0), (0, 0), (0, 1), (1, 0), (1, 1), (1, 1))[kind]
-        to = (xnb, ynb, sib, sib, sib, sib, (ynb, xnb)[half or 0])[kind]
+        to = (ynb, xnb)[half] if kind == 6 else (xnb, ynb, sib, sib, sib, sib)[kind]
         return pltpu.make_async_remote_copy(
             src_ref=xg.at[fh, g, ch, core, pairs(half)],
             dst_ref=xg.at[dh, g, dc, core, pairs(half)],
-            send_sem=send_sem.at[kind, g, half or 0],
-            recv_sem=recv_sem.at[dh, g, dc, core, half or 0],
+            send_sem=send_sem.at[kind, g, h0],
+            recv_sem=recv_sem.at[dh, g, dc, core, h0],
             device_id=to, device_id_type=pl.DeviceIdType.MESH)
 
     def arrived(fh, ch, k, g, half=None):
         ref = xg.at[fh, g, ch, k, pairs(half)]
-        pltpu.make_async_copy(ref, ref, recv_sem.at[fh, g, ch, k, half or 0]).wait()
+        pltpu.make_async_copy(ref, ref, recv_sem.at[fh, g, ch, k, 0 if half is None else half]).wait()
 
     def parts(g):
         return (None,) if g < 3 else (0, 1)
@@ -110,33 +111,26 @@
         send(2, g).start()
 
     def relay(g):
-        @pl.when(g < 3)
-        def _():
-            arrived(OWN, OTHER, core, g)
-            send(3, g).start()
-            send(6, g, 0).start()
-            arrived(OTHER, OWN, core, g)
-            send(4, g).start()
-            send(6, g, 1).start()
-            pl.when(g == 0)(lambda: direct_sends(2))
-            pl.when(g == 1)(lambda: direct_sends(3))
-            arrived(OWN, OTHER, 1 - core, g)
-            arrived(OTHER, OWN, 1 - core, g)
-
-        @pl.when(g == 3)
-        def _():
-            for half in range(2):
-                arrived(OWN, OTHER, core, g, half)
-                send(3, g, half).start()
-                if half == 0:
-                    send(6, g, 0).start()
-                arrived(OTHER, OWN, core, g, half)
-                send(4, g, half).start()
-                if half == 1:
-                    send(6, g, 1).start()
-            for half in range(2):
-                arrived(OWN, OTHER, 1 - core, g, half)
-                arrived(OTHER, OWN, 1 - core, g, half)
+        arrived(OWN, OTHER, core, g)
+        send(3, g).start()
+        send(6, g, 0).start()
+        arrived(OTHER, OWN, core, g)
+        send(4, g).start()
+        send(6, g, 1).start()
+        pl.when(g == 0)(lambda: direct_sends(2))
+        pl.when(g == 1)(lambda: direct_sends(3))
+        arrived(OWN, OTHER, 1 - core, g)
+        arrived(OTHER, OWN, 1 - core, g)
+
+    def relay_half(g, half):
+        arrived(OWN, OTHER, core, g, half)
+        send(3, g, half).start()
+        pl.when(half == 0)(lambda: send(6, g, 0).start())
+        arrived(OTHER, OWN, core, g, half)
+        send(4, g, half).start()
+        pl.when(half == 1)(lambda: send(6, g, 1).start())
+        arrived(OWN, OTHER, 1 - core, g, half)
+        arrived(OTHER, OWN, 1 - core, g, half)
 
     def relay_diag(g):
         for half in range(2):
@@ -195,20 +189,23 @@
             rt[fc * 2, r * HALF:(r + 1) * HALF, :] = t[:HALF]
             rt[fc * 2 + 1, r * HALF:(r + 1) * HALF, :] = t[HALF:]
 
-    def stage1(fh, ch, g, first):
+    def stage1(fh, ch, g, first, which=range(8)):
         xs = jnp.concatenate([
-            jnp.concatenate([xg[fh, g, ch, k, n] for n in range(8)], axis=1) for k in range(2)], axis=0)
+            jnp.concatenate([xg[fh, g, ch, k, n] for n in which], axis=1) for k in range(2)], axis=0)
         t = dot(l2[ch], xs)
         buf = g if fh == 0 else lax.rem(g + 4, 5)
-        if first:
-            t1r[buf] = t
-            return
-        for n in range(8):
-            lanes = slice(n * LANE, (n + 1) * LANE)
+        for i, n in enumerate(which):
+            lanes = slice(i * LANE, (i + 1) * LANE)
+            held = pl.ds(n * LANE if isinstance(n, int) else pl.multiple_of(n * LANE, LANE), LANE)
+            if first:
+                t1r[buf, :, held] = t[:, lanes]
+                continue
             for m in range(2):
-                v = [t[ab * LANE:(ab + 1) * LANE, lanes] + t1r[buf, ab * LANE:(ab + 1) * LANE, lanes] for ab in (2 * m, 2 * m + 1)]
+                v = [t[ab * LANE:(ab + 1) * LANE, lanes] + t1r[buf, ab * LANE:(ab + 1) * LANE, held] for ab in (2 * m, 2 * m + 1)]
                 for qb, w in enumerate(swap(*v)):
-                    t1g[:, (2 * n + qb) * 16:(2 * n + qb + 1) * 16, m * LANE:(m + 1) * LANE] = (w * scale[0:1, 0:1]).reshape(GROUPS, 16, LANE)
+                    row0 = (2 * n + qb) * 16
+                    row0 = row0 if isinstance(n, int) else pl.multiple_of(row0, 16)
+                    t1g[:, pl.ds(row0, 16), m * LANE:(m + 1) * LANE] = (w * scale[0:1, 0:1]).reshape(GROUPS, 16, LANE)
 
     def stage2(g):
         sc = scale[0:1, 0:1]
@@ -265,9 +262,22 @@
         stage2(g)
 
     def direct(g, _):
-        relay(g)
-        stage1(OWN, OTHER, g, False)
-        stage1(OTHER, OWN, g, True)
+        @pl.when(g < 3)
+        def _():
+            relay(g)
+            stage1(OWN, OTHER, g, False)
+            stage1(OTHER, OWN, g, True)
+
+        def halves(half, c):
+            relay_half(g, half)
+            which = [4 * half + n for n in range(4)]
+            stage1(OWN, OTHER, g, False, which)
+            stage1(OTHER, OWN, g, True, which)
+            return c
+
+        @pl.when(g == 3)
+        def _():
+            lax.fori_loop(0, 2, halves, 0)
         stage2(g)
         pl.when(g > 0)(lambda: relay_diag(g - 1))
         stage3(OWN, g)

time: 90.1 us -> 91.3 us (1.013)
  Pallas kernels: 86.6 us -> 87.8 us
    pallas_call x1, Pallas kernels: 86.6 us -> 87.8 us  [local_apply(): pl.pallas_call(kernel, out_shape=jax.ShapeDtypeStruct((128, 4, 4, 256), F...]
where the time goes in v9:
time: 91.3 us; the launch traced here: 91.1 us
  Pallas kernels  87.8 us (96%)
  local copies, waits for them, and re-layouts  3.33 us (4%)
    pallas_call x1, Pallas kernels, local_apply(): pl.pallas_call(kernel, out_shape=jax.ShapeDtypeStruct((128, 4, 4, 256), F...  87.8 us
    unnamed x1, local copies, waits for them, and re-layouts  3.33 us

profile of v9, /device:TPU:0, one launch (start us, length us, event | category | flops | bytes accessed | tf_op | source)
XLA Modules:
  0.0 91.1 jit_solution(9439091272853915988)
XLA Ops:
  0.0 87.8 %two_site.1 = f32[128,4,4,256]{3,2,1,0:T(4,128)} custom-call(f32[128,4,4,256]{3,2,1,0:T(4,128)} %x_ref.1, f32[128,4,512]{2,1,0:T(4,128)} %l_ref.1, f32[4,4,4,4]{3,2,1,0:T(4,128)} %w_hbm.1, f32[256,4,512]{2,1,0:T(4,128)} %r_ref.1), custom_call_target="tpu_custom_call" | custom-call | tf_op jit(solution)/shard_map/two_site/pallas_call | solution.py:314
  87.8 3.3 %copy.6 = f32[128,4,4,256]{3,2,1,0:T(4,128)} copy(f32[128,4,4,256]{3,2,1,0:T(4,128)} %two_site.1) | data formatting | bytes 4194304

commit v10 on v6

--- a/solution.py
+++ b/solution.py
@@ -70,18 +70,22 @@
         m = low[:v0.shape[0]]
         return jnp.where(m, v0, pltpu.roll(v1, HALF, 1)), jnp.where(m, pltpu.roll(v0, HALF, 1), v1)
 
-    def split(h):
-        for pq in range(16):
+    def split(h, half):
+        for pq in range(8 * half, 8 * half + 8):
             load(h, pq).wait()
-        for n in range(8):
+        for n in range(4 * half, 4 * half + 4):
             blocks = [(h * 16 + pq) for pq in (2 * n, 2 * n + 1)]
             v = [t1r[4, i // 8 * LANE:(i // 8 + 1) * LANE, i % 8 * LANE:(i % 8 + 1) * LANE] for i in blocks]
             xg[OWN, 2 * h, OWN, core, n], xg[OWN, 2 * h + 1, OWN, core, n] = swap(*v)
 
-    split(0)
+    split(0, 0)
     pl.semaphore_wait(barrier, 3)
-    for g in range(2):
-        direct_sends(g)
+    for half in range(2):
+        if half == 1:
+            split(0, 1)
+        for kind in range(2):
+            send(kind, 0, half).start()
+    direct_sends(1)
     for g in range(2):
         for half in range(2):
             send(2, g, half).start()
@@ -104,7 +108,8 @@
         cp.start()
 
 
-    split(1)
+    split(1, 0)
+    split(1, 1)
     for g in range(2, 4):
         for half in range(2):
             send(2, g, half).start()

time: 90.1 us -> 90 us (level)
  no operation moved by 1% of the time
where the time goes in v10:
time: 90 us; the launch traced here: 89.8 us
  Pallas kernels  86.5 us (96%)
  local copies, waits for them, and re-layouts  3.33 us (4%)
    pallas_call x1, Pallas kernels, local_apply(): pl.pallas_call(kernel, out_shape=jax.ShapeDtypeStruct((128, 4, 4, 256), F...  86.5 us
    unnamed x1, local copies, waits for them, and re-layouts  3.33 us

profile of v10, /device:TPU:0, one launch (start us, length us, event | category | flops | bytes accessed | tf_op | source)
XLA Modules:
  0.0 89.8 jit_solution(11499773920724217827)
XLA Ops:
  0.0 86.5 %two_site.1 = f32[128,4,4,256]{3,2,1,0:T(4,128)} custom-call(f32[128,4,4,256]{3,2,1,0:T(4,128)} %x_ref.1, f32[128,4,512]{2,1,0:T(4,128)} %l_ref.1, f32[4,4,4,4]{3,2,1,0:T(4,128)} %w_hbm.1, f32[256,4,512]{2,1,0:T(4,128)} %r_ref.1), custom_call_target="tpu_custom_call" | custom-call | tf_op jit(solution)/shard_map/two_site/pallas_call | solution.py:293
  86.5 3.3 %copy.6 = f32[128,4,4,256]{3,2,1,0:T(4,128)} copy(f32[128,4,4,256]{3,2,1,0:T(4,128)} %two_site.1) | data formatting | bytes 4194304
